TPU v7x, 32 devices: a whole 2x2x4 slice. The times are simulated.
32 devices in a mesh: groups: 2 (over y), dp: 4 (over x, core), tp: 4 (over z).
Axes of the slice: x: 2, y: 2, z: 4, core: 2. Of those that a mesh axis runs over, the one named last changes fastest.
Arguments:
- tokens: bfloat16 [256, 6144], P(('groups', 'tp'), 'dp'), parts along dimension 0, may hold values from -6 to 6
- gate_weight: bfloat16 [6144, 16384], P('dp', 'tp'), may hold values from -0.078125 to 0.078125
- up_weight: bfloat16 [6144, 16384], P('dp', 'tp'), may hold values from -0.078125 to 0.078125
- down_weight: bfloat16 [16384, 6144], P('tp', 'dp'), may hold values from -0.046875 to 0.046875
- expert_ids: int32 [256, 2], P(('groups', 'tp')), parts along dimension 0, may hold values from 0 to 7, as said below
- route_weights: float32 [256, 2], P(('groups', 'tp')), parts along dimension 0, may hold values from 0.1 to 1
Outputs:
- mixed: bfloat16 [256, 6144], P(('groups', 'tp'), 'dp'), parts along dimension 0
There are 2 independent parts, one for each index of `groups`. A program takes and returns all parts, laid end to end along the dimension named above; an argument that names none is the same for every part. Nothing has to cross between parts.
Inputs may be any that keep to these rules, and one draw needn't show every extreme that they name: `expert_ids`: each row names two different experts. Among the 32 rows of one index of tp, expert 0 is named by 1 to 16 rows, and by exactly 16 rows on at least one index of tp.
All inputs are finite; a program needn't handle non-finite values.
Results may differ from a plain program's by a relative error of at most 0.03.
Values may be sent and summed in bfloat16 or wider, within the bound.
No kernel may reach another device: no remote copies, remote signals or barrier semaphores. Data moves between devices by JAX's collectives and lax.ppermute only.
A program may use at most 64 MiB of HBM per device.

v0:
```python
import functools

import jax
import jax.numpy as jnp
from jax import lax
from jax.experimental import pallas as pl
from jax.experimental.pallas import tpu as pltpu
from jax.sharding import PartitionSpec as P


MOST = 16
F32 = jnp.float32
BF16 = jnp.bfloat16
PRIOR = 100000
WIDE = 2048
CUTS = (0, 4, 8, 12, 16)
GRANT = 2 * 1024 * 1024
VM = pl.BlockSpec(memory_space=pltpu.VMEM)


def call(body, outs, flops, nbytes, *args, scratch=(), spec=VM):
    return pl.pallas_call(
        body,
        out_shape=outs,
        in_specs=[spec] * len(args),
        out_specs=jax.tree.map(lambda _: VM, outs),
        scratch_shapes=scratch,
        compiler_params=pltpu.CompilerParams(vmem_limit_bytes=GRANT),
        cost_estimate=pl.CostEstimate(flops=flops, bytes_accessed=nbytes, transcendentals=0),
    )(*args)


def shape(dims, dtype):
    return jax.ShapeDtypeStruct(dims, dtype)


def in_vmem(array):
    return pltpu.with_memory_space_constraint(array, pltpu.VMEM)


def in_hbm(array):
    return pltpu.with_memory_space_constraint(array, pltpu.HBM)


def slots(ids_t, columns):
    count = ids_t.shape[1]
    held = jnp.max(jnp.where(ids_t == 0, 1.0, 0.0), axis=0, keepdims=True)
    row = lax.broadcasted_iota(jnp.int32, (count, count), 0)
    col = lax.broadcasted_iota(jnp.int32, (count, count), 1)
    spread = jnp.broadcast_to(held, (count, count))
    rank = jnp.sum(jnp.where(col < row, spread, 0.0), axis=1, keepdims=True)
    routed = jnp.sum(jnp.where(col == row, spread, 0.0), axis=1, keepdims=True)
    slot = (lax.broadcasted_iota(jnp.int32, (count, columns), 1) % MOST).astype(F32)
    return jnp.where((slot == rank) & (routed > 0.0), 1.0, 0.0).astype(BF16)


def pack_body(ids_hbm, tokens_hbm, out_ref, ids_ref, tokens_ref, sems):
    copies = [
        pltpu.make_async_copy(ids_hbm, ids_ref, sems.at[0]),
        pltpu.make_async_copy(tokens_hbm, tokens_ref, sems.at[1]),
    ]
    for copy in copies:
        copy.start()
    copies[0].wait()
    one_hot = slots(ids_ref[...], MOST)
    copies[1].wait()
    out_ref[...] = lax.dot_general(
        one_hot, tokens_ref[...], (((0,), (0,)), ((), ())), preferred_element_type=F32
    ).astype(BF16)


def bit_order(spot):
    return (spot % 2) * 2 + spot // 2


def gather_body(*refs):
    out_ref = refs[-1]
    place = (lax.axis_index("dp") % 2) ^ lax.axis_index("tp")
    for q, block in enumerate(refs[:-1]):
        spot = bit_order(place ^ q)
        out_ref[pl.ds(pl.multiple_of(spot * MOST, MOST), MOST), :] = block[...]


def gate_up(rows, weights, keep_ref, send_ref, low, high):
    half = rows.shape[0] // 2
    for k, weight in enumerate(weights):
        for at in range(low, high, WIDE):
            to = min(at + WIDE, high)
            part = jnp.dot(rows, weight[:, at:to], preferred_element_type=F32).astype(BF16)
            keep_ref[k, :, at - low : to - low] = part[:half]
            send_ref[k, :, at - low : to - low] = part[half:]


def first_body(low, high, *refs):
    blocks = refs[:-5]
    gate_ref, up_ref, keep_ref, send_ref, rows_ref = refs[-5:]
    gather_body(*blocks, rows_ref)
    gate_up(rows_ref[...], (gate_ref, up_ref), keep_ref, send_ref, low, high)


def later_body(low, high, rows_ref, gate_ref, up_ref, keep_ref, send_ref):
    gate_up(rows_ref[...], (gate_ref, up_ref), keep_ref, send_ref, low, high)


def fold_body(keep_ref, got_ref, own_ref, send_ref):
    total = keep_ref[...].astype(F32) + got_ref[...].astype(F32)
    own_ref[...] = total
    send_ref[...] = total.astype(BF16)


def hidden_body(own_ref, got_ref, out_ref):
    total = own_ref[...] + got_ref[...].astype(F32)
    gate, up = total[0], total[1]
    out_ref[...] = (gate / (1.0 + jnp.exp(-gate)) * up).astype(BF16)


def down_body(low, high, mine_ref, beside_ref, weight_ref, *refs):
    hidden = jnp.concatenate([mine_ref[...], beside_ref[...]], axis=0)
    value = jnp.dot(hidden, weight_ref[low:high, :], preferred_element_type=F32)
    refs[-1][...] = value + refs[0][...] if len(refs) > 1 else value


def last_body(n_tp, low, high, mine_ref, beside_ref, weight_ref, total_ref, own_ref, *refs):
    sends, scratch = refs[:-1], refs[-1]
    down_body(low, high, mine_ref, beside_ref, weight_ref, total_ref, scratch)
    place = (lax.axis_index("dp") % 2) ^ lax.axis_index("tp")
    for q in range(n_tp):
        block = scratch[pl.ds(pl.multiple_of(bit_order(place ^ q) * MOST, MOST), MOST), :]
        if q == 0:
            own_ref[...] = block
        else:
            sends[q - 1][...] = block.astype(BF16)


def final_body(ids_ref, route_ref, own_ref, *refs):
    out_ref = refs[-1]
    own = own_ref[...]
    high = own.astype(BF16)
    rest = own - high.astype(F32)
    mid = rest.astype(BF16)
    low = (rest - mid.astype(F32)).astype(BF16)
    terms = jnp.concatenate([high, mid, low] + [got[...] for got in refs[:-1]], axis=0)
    ids = ids_ref[...]
    count = ids.shape[1]
    held = jnp.sum(jnp.where(ids == 0, route_ref[...], 0.0), axis=0, keepdims=True)
    row = lax.broadcasted_iota(jnp.int32, (count, count), 0)
    col = lax.broadcasted_iota(jnp.int32, (count, count), 1)
    combine = jnp.sum(
        jnp.where(col == row, jnp.broadcast_to(held, (count, count)), 0.0), axis=1, keepdims=True
    )
    spread = jnp.dot(slots(ids, terms.shape[0]), terms, preferred_element_type=F32)
    out_ref[...] = (combine * spread).astype(BF16)


def swap(value, axis, size, mask):
    return lax.ppermute(value, axis, [(i, i ^ mask) for i in range(size)])


def direct(n_dp, n_tp, tokens, gate_weight, up_weight, down_weight, expert_ids, route_weights):
    ids_t, route_t = expert_ids.T, route_weights.T
    model, width = gate_weight.shape
    out_width = down_weight.shape[1]
    total = MOST * n_tp
    gate_weight, up_weight, down_weight = map(in_vmem, (gate_weight, up_weight, down_weight))
    packed = call(
        pack_body,
        shape((MOST, model), BF16),
        PRIOR * total * model * width,
        PRIOR * model * width,
        in_hbm(ids_t),
        in_hbm(tokens),
        scratch=[
            pltpu.VMEM(ids_t.shape, ids_t.dtype),
            pltpu.VMEM(tokens.shape, tokens.dtype),
            pltpu.SemaphoreType.DMA((2,)),
        ],
        spec=pl.BlockSpec(memory_space=pltpu.HBM),
    )
    blocks = [packed]
    for q in range(1, n_tp):
        blocks.append(swap(packed, "tp", n_tp, q))
    cuts = [width * cut // 16 for cut in CUTS]
    spans = list(zip(cuts[:-1], cuts[1:]))
    folded = []
    for c, (low, high) in enumerate(spans):
        dims = (2, total // 2, high - low)
        cost = 4 * total * model * (high - low), 4 * model * (high - low)
        if c == 0:
            keep, send, rows = call(
                functools.partial(first_body, low, high),
                [shape(dims, BF16)] * 2 + [shape((total, model), BF16)],
                *cost,
                *blocks,
                gate_weight,
                up_weight,
            )
        else:
            keep, send = call(
                functools.partial(later_body, low, high),
                [shape(dims, BF16)] * 2,
                *cost,
                rows,
                gate_weight,
                up_weight,
            )
        got = swap(send, "dp", n_dp, 1)
        folded.append(
            call(fold_body, [shape(dims, F32), shape(dims, BF16)], total * width, 6 * total * width, keep, got)
        )
    value = []
    for c, (low, high) in enumerate(spans):
        own, send = folded[c]
        got = swap(send, "dp", n_dp, 2)
        mine = call(
            hidden_body, shape(own.shape[1:], BF16), total * width, 3 * total * width, own, got
        )
        beside = swap(mine, "dp", n_dp, 1)
        cost = 2 * total * (high - low) * out_width, 2 * (high - low) * out_width
        last = c == len(spans) - 1
        value = call(
            functools.partial(last_body, n_tp, low, high) if last else functools.partial(down_body, low, high),
            [shape((MOST, out_width), F32)] + [shape((MOST, out_width), BF16)] * (n_tp - 1)
            if last
            else [shape((total, out_width), F32)],
            *cost,
            mine,
            beside,
            down_weight,
            *value,
            scratch=[pltpu.VMEM((total, out_width), F32)] if last else (),
        )
    own, *sends = value
    got = []
    for q, send in enumerate(sends):
        got.append(swap(send, "tp", n_tp, q + 1))
    return call(
        final_body, shape((tokens.shape[0], out_width), BF16), 2 * tokens.size, 4 * tokens.size,
        ids_t, route_t, own, *got,
    )


def general(tokens, gate_weight, up_weight, down_weight, expert_ids, route_weights):
    held_mask = expert_ids == 0
    combine = jnp.sum(jnp.where(held_mask, route_weights, jnp.zeros_like(route_weights)), axis=1)
    hidden_width = gate_weight.shape[1]
    routed = jnp.any(held_mask, axis=1)
    slot_rank = jnp.cumsum(routed.astype(jnp.int32)) - 1
    slot_ids = jnp.arange(MOST, dtype=jnp.int32)
    dispatch = ((slot_rank[None, :] == slot_ids[:, None]) & routed[None, :]).astype(BF16)
    packed = jnp.dot(dispatch, tokens, preferred_element_type=F32).astype(BF16)
    row_block = lax.all_gather(packed, "tp", axis=0, tiled=True)
    gate_part = jnp.dot(row_block, gate_weight, preferred_element_type=F32).astype(BF16)
    up_part = jnp.dot(row_block, up_weight, preferred_element_type=F32).astype(BF16)
    gate_up = jnp.concatenate([gate_part, up_part], axis=1)
    summed = lax.psum(gate_up, "dp").astype(F32)
    hidden = (jax.nn.silu(summed[:, :hidden_width]) * summed[:, hidden_width:]).astype(BF16)
    partial_value = jnp.dot(hidden, down_weight, preferred_element_type=F32)
    result = jnp.dot(
        dispatch.T.astype(F32),
        lax.psum_scatter(
            partial_value.astype(BF16), "tp", scatter_dimension=0, tiled=True
        ).astype(F32),
        precision=lax.Precision.HIGHEST,
    )
    return (combine[:, None] * result).astype(BF16)


def solution(mesh):
    n_dp, n_tp = mesh.shape["dp"], mesh.shape["tp"]
    in_specs = (
        P(("groups", "tp"), "dp"),
        P("dp", "tp"),
        P("dp", "tp"),
        P("tp", "dp"),
        P(("groups", "tp"), None),
        P(("groups", "tp"), None),
    )
    out_specs = P(("groups", "tp"), "dp")
    def specialised(*args):
        return direct(n_dp, n_tp, *args)

    fits = n_dp == n_tp == 4
    return jax.shard_map(
        specialised if fits else general,
        mesh=mesh,
        in_specs=in_specs,
        out_specs=out_specs,
        check_vma=False,
    )
```

profile of v0, /device:TPU:0, one launch (start us, length us, event | category | flops | bytes accessed | tf_op | source)
XLA Modules:
  0.0 44.5 jit_solution(14267785637860433410)
XLA Ops:
  0.0 1.3 %shard_map.64.refs_0_ = bf16[16,1536]{1,0:T(8,128)(2,1)S(1)} custom-call(s32[2,32]{1,0:T(2,128)} %bitcast.4, bf16[32,1536]{1,0:T(8,128)(2,1)} %tokens_hbm.1), custom_call_target="tpu_custom_call" | custom-call | flops 40265318400000 | bytes 629145600000 | tf_op jit(solution)/shard_map/pallas_call | solution.py:22
  1.3 3.1 %collective-permute-start = (bf16[16,1536]{1,0:T(8,128)(2,1)S(1)}, bf16[16,1536]{1,0:T(8,128)(2,1)S(1)}, u32[]{:S(2)}, u32[]{:S(2)}) collective-permute-start(bf16[16,1536]{1,0:T(8,128)(2,1)S(1)} %shard_map.64.refs_0_), channel_id=1, source_target_pairs={{0,1},{1,0},{2,3},{3,2},{4,5},{5,4},{6,7},{7,6},{8,9},{9,8},{10,11... | collective-permute-start | bytes 147464 | tf_op jit(solution)/shard_map/ppermute | solution.py:156
  4.4 2.6 %collective-permute-start.1 = (bf16[16,1536]{1,0:T(8,128)(2,1)S(1)}, bf16[16,1536]{1,0:T(8,128)(2,1)S(1)}, u32[]{:S(2)}, u32[]{:S(2)}) collective-permute-start(bf16[16,1536]{1,0:T(8,128)(2,1)S(1)} %shard_map.64.refs_0_), channel_id=1, source_target_pairs={{0,2},{1,3},{2,0},{3,1},{4,6},{5,7},{6,4},{7,5},{8,10},{9,11},{10,... | collective-permute-start | bytes 147464 | tf_op jit(solution)/shard_map/ppermute | solution.py:156
  7.0 0.0 collective-permute-start.2
  7.0 0.0 collective-permute-done.refs_1_
  7.0 3.3 %collective-permute-done.1.refs_2_ = bf16[16,1536]{1,0:T(8,128)(2,1)S(1)} collective-permute-done((bf16[16,1536]{1,0:T(8,128)(2,1)S(1)}, bf16[16,1536]{1,0:T(8,128)(2,1)S(1)}, u32[]{:S(2)}, u32[]{:S(2)}) %collective-permute-start.1) | collective-permute-done | bytes 49184 | tf_op jit(solution)/shard_map/ppermute | solution.py:156
  10.3 2.6 %collective-permute-done.2.refs_3_ = bf16[16,1536]{1,0:T(8,128)(2,1)S(1)} collective-permute-done((bf16[16,1536]{1,0:T(8,128)(2,1)S(1)}, bf16[16,1536]{1,0:T(8,128)(2,1)S(1)}, u32[]{:S(2)}, u32[]{:S(2)}) %collective-permute-start.2) | collective-permute-done | bytes 49184 | tf_op jit(solution)/shard_map/ppermute | solution.py:156
  12.9 1.2 %shard_map.65 = (bf16[2,32,1024]{2,1,0:T(8,128)(2,1)S(1)}, bf16[2,32,1024]{2,1,0:T(8,128)(2,1)S(1)}, bf16[64,1536]{1,0:T(8,128)(2,1)S(1)}) custom-call(bf16[16,1536]{1,0:T(8,128)(2,1)S(1)} %shard_map.64.refs_0_, bf16[16,1536]{1,0:T(8,128)(2,1)S(1)} %collective-permute-done.refs_1_, bf16[16,1536]{1,0:T(8,128)(2,1)S(1)} %collective-permute-done.1.refs_2_, ...), custom_call_target="tpu_custom_call" | custom-call | flops 402653184 | bytes 6291456 | tf_op jit(solution)/shard_map/pallas_call | solution.py:22
  14.1 0.1 collective-permute-start.12
  14.2 1.2 %shard_map.72 = (bf16[2,32,1024]{2,1,0:T(8,128)(2,1)S(1)}, bf16[2,32,1024]{2,1,0:T(8,128)(2,1)S(1)}) custom-call(bf16[64,1536]{1,0:T(8,128)(2,1)S(1)} %get-tuple-element.26.rows_ref, bf16[1536,4096]{1,0:T(8,128)(2,1)S(1)} %copy-done, bf16[1536,4096]{1,0:T(8,128)(2,1)S(1)} %copy-done.1), custom_call_target="tpu_custom_call" | custom-call | flops 402653184 | bytes 6291456 | tf_op jit(solution)/shard_map/pallas_call | solution.py:22
  15.4 0.0 slice-start
  15.4 0.0 slice-start.1
  15.4 1.2 %shard_map.69 = (bf16[2,32,1024]{2,1,0:T(8,128)(2,1)S(1)}, bf16[2,32,1024]{2,1,0:T(8,128)(2,1)S(1)}) custom-call(bf16[64,1536]{1,0:T(8,128)(2,1)S(1)} %get-tuple-element.26.rows_ref, bf16[1536,4096]{1,0:T(8,128)(2,1)S(1)} %copy-done, bf16[1536,4096]{1,0:T(8,128)(2,1)S(1)} %copy-done.1), custom_call_target="tpu_custom_call" | custom-call | flops 402653184 | bytes 6291456 | tf_op jit(solution)/shard_map/pallas_call | solution.py:22
  16.6 0.0 slice-start.2
  16.6 0.6 %collective-permute-start.9 = (bf16[2,32,1024]{2,1,0:T(8,128)(2,1)S(1)}, bf16[2,32,1024]{2,1,0:T(8,128)(2,1)S(1)}, u32[]{:S(2)}, u32[]{:S(2)}) collective-permute-start(bf16[2,32,1024]{2,1,0:T(8,128)(2,1)S(1)} %get-tuple-element.36), channel_id=1, source_target_pairs={{0,4},{4,0},{8,12},{12,8},{1,5},{5,1},{9,13},{13,9},{2,6},{6,2},{1... | collective-permute-start | bytes 393224 | tf_op jit(solution)/shard_map/ppermute | solution.py:156
  17.2 0.1 collective-permute-start.6
  17.2 1.2 %shard_map.66 = (bf16[2,32,1024]{2,1,0:T(8,128)(2,1)S(1)}, bf16[2,32,1024]{2,1,0:T(8,128)(2,1)S(1)}) custom-call(bf16[64,1536]{1,0:T(8,128)(2,1)S(1)} %get-tuple-element.26.rows_ref, bf16[1536,4096]{1,0:T(8,128)(2,1)S(1)} %copy-done, bf16[1536,4096]{1,0:T(8,128)(2,1)S(1)} %copy-done.1), custom_call_target="tpu_custom_call" | custom-call | flops 402653184 | bytes 6291456 | tf_op jit(solution)/shard_map/pallas_call | solution.py:22
  18.4 0.5 %collective-permute-start.3 = (bf16[2,32,1024]{2,1,0:T(8,128)(2,1)S(1)}, bf16[2,32,1024]{2,1,0:T(8,128)(2,1)S(1)}, u32[]{:S(2)}, u32[]{:S(2)}) collective-permute-start(bf16[2,32,1024]{2,1,0:T(8,128)(2,1)S(1)} %get-tuple-element.28), channel_id=1, source_target_pairs={{0,4},{4,0},{8,12},{12,8},{1,5},{5,1},{9,13},{13,9},{2,6},{6,2},{1... | collective-permute-start | bytes 393224 | tf_op jit(solution)/shard_map/ppermute | solution.py:156
  18.9 0.0 collective-permute-done.12.got_ref
  19.0 1.6 %collective-permute-start.13 = (bf16[2,32,1024]{2,1,0:T(8,128)(2,1)S(1)}, bf16[2,32,1024]{2,1,0:T(8,128)(2,1)S(1)}, u32[]{:S(2)}, u32[]{:S(2)}) collective-permute-start(bf16[2,32,1024]{2,1,0:T(8,128)(2,1)S(1)} %get-tuple-element.42), channel_id=1, source_target_pairs={{0,8},{4,12},{8,0},{12,4},{1,9},{5,13},{9,1},{13,5},{2,10},{6,14},... | collective-permute-start | bytes 393224 | tf_op jit(solution)/shard_map/ppermute | solution.py:156
  20.5 0.0 collective-permute-done.9.got_ref
  20.6 0.6 %collective-permute-start.10 = (bf16[2,32,1024]{2,1,0:T(8,128)(2,1)S(1)}, bf16[2,32,1024]{2,1,0:T(8,128)(2,1)S(1)}, u32[]{:S(2)}, u32[]{:S(2)}) collective-permute-start(bf16[2,32,1024]{2,1,0:T(8,128)(2,1)S(1)} %get-tuple-element.38), channel_id=1, source_target_pairs={{0,8},{4,12},{8,0},{12,4},{1,9},{5,13},{9,1},{13,5},{2,10},{6,14},... | collective-permute-start | bytes 393224 | tf_op jit(solution)/shard_map/ppermute | solution.py:156
  21.2 0.0 collective-permute-done.6.got_ref
  21.2 1.6 %collective-permute-start.7 = (bf16[2,32,1024]{2,1,0:T(8,128)(2,1)S(1)}, bf16[2,32,1024]{2,1,0:T(8,128)(2,1)S(1)}, u32[]{:S(2)}, u32[]{:S(2)}) collective-permute-start(bf16[2,32,1024]{2,1,0:T(8,128)(2,1)S(1)} %get-tuple-element.34), channel_id=1, source_target_pairs={{0,8},{4,12},{8,0},{12,4},{1,9},{5,13},{9,1},{13,5},{2,10},{6,14},... | collective-permute-start | bytes 393224 | tf_op jit(solution)/shard_map/ppermute | solution.py:156
  22.8 0.6 %collective-permute-start.4 = (bf16[2,32,1024]{2,1,0:T(8,128)(2,1)S(1)}, bf16[2,32,1024]{2,1,0:T(8,128)(2,1)S(1)}, u32[]{:S(2)}, u32[]{:S(2)}) collective-permute-start(bf16[2,32,1024]{2,1,0:T(8,128)(2,1)S(1)} %get-tuple-element.30), channel_id=1, source_target_pairs={{0,8},{4,12},{8,0},{12,4},{1,9},{5,13},{9,1},{13,5},{2,10},{6,14},... | collective-permute-start | bytes 393224 | tf_op jit(solution)/shard_map/ppermute | solution.py:156
  23.4 2.0 %collective-permute-done.13.got_ref = bf16[2,32,1024]{2,1,0:T(8,128)(2,1)S(1)} collective-permute-done((bf16[2,32,1024]{2,1,0:T(8,128)(2,1)S(1)}, bf16[2,32,1024]{2,1,0:T(8,128)(2,1)S(1)}, u32[]{:S(2)}, u32[]{:S(2)}) %collective-permute-start.13) | collective-permute-done | bytes 131104 | tf_op jit(solution)/shard_map/ppermute | solution.py:156
  25.4 0.1 shard_map.76.mine_ref
  25.5 0.1 collective-permute-start.14
  25.6 2.7 %collective-permute-done.10.got_ref = bf16[2,32,1024]{2,1,0:T(8,128)(2,1)S(1)} collective-permute-done((bf16[2,32,1024]{2,1,0:T(8,128)(2,1)S(1)}, bf16[2,32,1024]{2,1,0:T(8,128)(2,1)S(1)}, u32[]{:S(2)}, u32[]{:S(2)}) %collective-permute-start.10) | collective-permute-done | bytes 131104 | tf_op jit(solution)/shard_map/ppermute | solution.py:156
  28.2 0.1 shard_map.74.mine_ref
  28.3 0.1 collective-permute-start.11
  28.4 2.7 %collective-permute-done.7.got_ref = bf16[2,32,1024]{2,1,0:T(8,128)(2,1)S(1)} collective-permute-done((bf16[2,32,1024]{2,1,0:T(8,128)(2,1)S(1)}, bf16[2,32,1024]{2,1,0:T(8,128)(2,1)S(1)}, u32[]{:S(2)}, u32[]{:S(2)}) %collective-permute-start.7) | collective-permute-done | bytes 131104 | tf_op jit(solution)/shard_map/ppermute | solution.py:156
  31.0 0.1 shard_map.71.mine_ref
  31.1 0.1 collective-permute-start.8
  31.2 1.8 %collective-permute-done.4.got_ref = bf16[2,32,1024]{2,1,0:T(8,128)(2,1)S(1)} collective-permute-done((bf16[2,32,1024]{2,1,0:T(8,128)(2,1)S(1)}, bf16[2,32,1024]{2,1,0:T(8,128)(2,1)S(1)}, u32[]{:S(2)}, u32[]{:S(2)}) %collective-permute-start.4) | collective-permute-done | bytes 131104 | tf_op jit(solution)/shard_map/ppermute | solution.py:156
  33.0 0.1 shard_map.68.mine_ref
  33.0 0.1 collective-permute-start.5
  33.2 0.6 %shard_map.77.refs_0_ = f32[64,1536]{1,0:T(8,128)S(1)} custom-call(bf16[32,1024]{1,0:T(8,128)(2,1)S(1)} %shard_map.76.mine_ref, bf16[32,1024]{1,0:T(8,128)(2,1)S(1)} %collective-permute-done.14.beside_ref, bf16[4096,1536]{1,0:T(8,128)(2,1)S(1)} %bitcast.3), custom_call_target="tpu_custom_call" | custom-call | flops 201326592 | bytes 3145728 | tf_op jit(solution)/shard_map/pallas_call | solution.py:22
  33.8 0.7 %shard_map.78.refs_0_ = f32[64,1536]{1,0:T(8,128)S(1)} custom-call(bf16[32,1024]{1,0:T(8,128)(2,1)S(1)} %shard_map.74.mine_ref, bf16[32,1024]{1,0:T(8,128)(2,1)S(1)} %collective-permute-done.11.beside_ref, bf16[4096,1536]{1,0:T(8,128)(2,1)S(1)} %bitcast.3, f32[64,1536]{1,0:T(8,128)S(1)} %shard_map.77.refs_0_), custom_call_target="tpu_custom_call" | custom-call | flops 201326592 | bytes 3145728 | tf_op jit(solution)/shard_map/pallas_call | solution.py:22
  34.5 0.0 copy-start.2
  34.5 0.0 copy-start.3
  34.5 0.7 %shard_map.79.total_ref = f32[64,1536]{1,0:T(8,128)S(1)} custom-call(bf16[32,1024]{1,0:T(8,128)(2,1)S(1)} %shard_map.71.mine_ref, bf16[32,1024]{1,0:T(8,128)(2,1)S(1)} %collective-permute-done.8.beside_ref, bf16[4096,1536]{1,0:T(8,128)(2,1)S(1)} %bitcast.3, f32[64,1536]{1,0:T(8,128)S(1)} %shard_map.78.refs_0_), custom_call_target="tpu_custom_call" | custom-call | flops 201326592 | bytes 3145728 | tf_op jit(solution)/shard_map/pallas_call | solution.py:22
  35.2 0.7 %shard_map.80 = (f32[16,1536]{1,0:T(8,128)S(1)}, bf16[16,1536]{1,0:T(8,128)(2,1)S(1)}, bf16[16,1536]{1,0:T(8,128)(2,1)S(1)}, bf16[16,1536]{1,0:T(8,128)(2,1)S(1)}) custom-call(bf16[32,1024]{1,0:T(8,128)(2,1)S(1)} %shard_map.68.mine_ref, bf16[32,1024]{1,0:T(8,128)(2,1)S(1)} %collective-permute-done.5.beside_ref, bf16[4096,1536]{1,0:T(8,128)(2,1)S(1)} %bitcast.3, ...), custom_call_target="tpu_custom_call" | custom-call | flops 201326592 | bytes 3145728 | tf_op jit(solution)/shard_map/pallas_call | solution.py:22
  35.9 0.1 collective-permute-start.15
  36.0 1.3 %collective-permute-start.16 = (bf16[16,1536]{1,0:T(8,128)(2,1)S(1)}, bf16[16,1536]{1,0:T(8,128)(2,1)S(1)}, u32[]{:S(2)}, u32[]{:S(2)}) collective-permute-start(bf16[16,1536]{1,0:T(8,128)(2,1)S(1)} %get-tuple-element.45), channel_id=1, source_target_pairs={{0,2},{1,3},{2,0},{3,1},{4,6},{5,7},{6,4},{7,5},{8,10},{9,11},{10,... | collective-permute-start | bytes 147464 | tf_op jit(solution)/shard_map/ppermute | solution.py:156
  37.3 3.1 %collective-permute-start.17 = (bf16[16,1536]{1,0:T(8,128)(2,1)S(1)}, bf16[16,1536]{1,0:T(8,128)(2,1)S(1)}, u32[]{:S(2)}, u32[]{:S(2)}) collective-permute-start(bf16[16,1536]{1,0:T(8,128)(2,1)S(1)} %get-tuple-element.46), channel_id=1, source_target_pairs={{0,3},{1,2},{2,1},{3,0},{4,7},{5,6},{6,5},{7,4},{8,11},{9,10},{10,... | collective-permute-start | bytes 147464 | tf_op jit(solution)/shard_map/ppermute | solution.py:156
  40.3 3.3 %collective-permute-done.16.refs_1_ = bf16[16,1536]{1,0:T(8,128)(2,1)S(1)} collective-permute-done((bf16[16,1536]{1,0:T(8,128)(2,1)S(1)}, bf16[16,1536]{1,0:T(8,128)(2,1)S(1)}, u32[]{:S(2)}, u32[]{:S(2)}) %collective-permute-start.16) | collective-permute-done | bytes 49184 | tf_op jit(solution)/shard_map/ppermute | solution.py:156
  43.7 0.9 %shard_map.81 = bf16[32,1536]{1,0:T(8,128)(2,1)} custom-call(s32[2,32]{1,0:T(2,128)S(1)} %bitcast.5, f32[2,32]{1,0:T(2,128)S(1)} %bitcast.6, f32[16,1536]{1,0:T(8,128)S(1)} %get-tuple-element.43.own_ref, bf16[16,1536]{1,0:T(8,128)(2,1)S(1)} %collective-permute-done.15.refs_0_, bf16[16,1536]{1,0:T(8,128)(2,1)S(1)} %collective-permute-done.16.refs_1_, ...), custom_call_target="tpu_custom_call" | custom-call | flops 98304 | bytes 196608 | tf_op jit(solution)/shard_map/pallas_call | solution.py:22
  (21 shorter events, 0.2 us)
Async XLA Ops:
  0.0 12.9 %copy-start = (bf16[1536,4096]{1,0:T(8,128)(2,1)S(1)}, bf16[1536,4096]{1,0:T(8,128)(2,1)}, u32[]{:S(2)}) copy-start(bf16[1536,4096]{1,0:T(8,128)(2,1)} %gate_ref.5) | copy-start | bytes 37748740
  0.0 12.9 %copy-start.1 = (bf16[1536,4096]{1,0:T(8,128)(2,1)S(1)}, bf16[1536,4096]{1,0:T(8,128)(2,1)}, u32[]{:S(2)}) copy-start(bf16[1536,4096]{1,0:T(8,128)(2,1)} %up_ref.5) | copy-start | bytes 37748740
  1.3 5.7 %collective-permute-start = (bf16[16,1536]{1,0:T(8,128)(2,1)S(1)}, bf16[16,1536]{1,0:T(8,128)(2,1)S(1)}, u32[]{:S(2)}, u32[]{:S(2)}) collective-permute-start(bf16[16,1536]{1,0:T(8,128)(2,1)S(1)} %shard_map.64.refs_0_), channel_id=1, source_target_pairs={{0,1},{1,0},{2,3},{3,2},{4,5},{5,4},{6,7},{7,6},{8,9},{9,8},{10,11... | collective-permute-start | bytes 147464 | tf_op jit(solution)/shard_map/ppermute | solution.py:156
  4.4 5.9 %collective-permute-start.1 = (bf16[16,1536]{1,0:T(8,128)(2,1)S(1)}, bf16[16,1536]{1,0:T(8,128)(2,1)S(1)}, u32[]{:S(2)}, u32[]{:S(2)}) collective-permute-start(bf16[16,1536]{1,0:T(8,128)(2,1)S(1)} %shard_map.64.refs_0_), channel_id=1, source_target_pairs={{0,2},{1,3},{2,0},{3,1},{4,6},{5,7},{6,4},{7,5},{8,10},{9,11},{10,... | collective-permute-start | bytes 147464 | tf_op jit(solution)/shard_map/ppermute | solution.py:156
  7.0 5.9 %collective-permute-start.2 = (bf16[16,1536]{1,0:T(8,128)(2,1)S(1)}, bf16[16,1536]{1,0:T(8,128)(2,1)S(1)}, u32[]{:S(2)}, u32[]{:S(2)}) collective-permute-start(bf16[16,1536]{1,0:T(8,128)(2,1)S(1)} %shard_map.64.refs_0_), channel_id=1, source_target_pairs={{0,3},{1,2},{2,1},{3,0},{4,7},{5,6},{6,5},{7,4},{8,11},{9,10},{10,... | collective-permute-start | bytes 147464 | tf_op jit(solution)/shard_map/ppermute | solution.py:156
  14.1 4.9 %collective-permute-start.12 = (bf16[2,32,1024]{2,1,0:T(8,128)(2,1)S(1)}, bf16[2,32,1024]{2,1,0:T(8,128)(2,1)S(1)}, u32[]{:S(2)}, u32[]{:S(2)}) collective-permute-start(bf16[2,32,1024]{2,1,0:T(8,128)(2,1)S(1)} %get-tuple-element.40), channel_id=1, source_target_pairs={{0,4},{4,0},{8,12},{12,8},{1,5},{5,1},{9,13},{13,9},{2,6},{6,2},{1... | collective-permute-start | bytes 393224 | tf_op jit(solution)/shard_map/ppermute | solution.py:156
  15.4 17.8 %slice-start = ((s8[12582912]{0:T(1024)(128)(4,1)}), s8[4194304]{0:T(1024)(128)(4,1)S(1)}, s32[]{:S(2)}) async-start(s8[12582912]{0:T(1024)(128)(4,1)} %bitcast.2), calls=%async_computation | async-start | bytes 8388608
  15.4 17.8 %slice-start.1 = ((s8[12582912]{0:T(1024)(128)(4,1)}), s8[4194304]{0:T(1024)(128)(4,1)S(1)}, s32[]{:S(2)}) async-start(s8[12582912]{0:T(1024)(128)(4,1)} %bitcast.2), calls=%async_computation.1 | async-start | bytes 8388608
  16.6 16.6 %slice-start.2 = ((s8[12582912]{0:T(1024)(128)(4,1)}), s8[4194304]{0:T(1024)(128)(4,1)S(1)}, s32[]{:S(2)}) async-start(s8[12582912]{0:T(1024)(128)(4,1)} %bitcast.2), calls=%async_computation.2 | async-start | bytes 8388608
  16.6 3.9 %collective-permute-start.9 = (bf16[2,32,1024]{2,1,0:T(8,128)(2,1)S(1)}, bf16[2,32,1024]{2,1,0:T(8,128)(2,1)S(1)}, u32[]{:S(2)}, u32[]{:S(2)}) collective-permute-start(bf16[2,32,1024]{2,1,0:T(8,128)(2,1)S(1)} %get-tuple-element.36), channel_id=1, source_target_pairs={{0,4},{4,0},{8,12},{12,8},{1,5},{5,1},{9,13},{13,9},{2,6},{6,2},{1... | collective-permute-start | bytes 393224 | tf_op jit(solution)/shard_map/ppermute | solution.py:156
  17.2 4.0 %collective-permute-start.6 = (bf16[2,32,1024]{2,1,0:T(8,128)(2,1)S(1)}, bf16[2,32,1024]{2,1,0:T(8,128)(2,1)S(1)}, u32[]{:S(2)}, u32[]{:S(2)}) collective-permute-start(bf16[2,32,1024]{2,1,0:T(8,128)(2,1)S(1)} %get-tuple-element.32), channel_id=1, source_target_pairs={{0,4},{4,0},{8,12},{12,8},{1,5},{5,1},{9,13},{13,9},{2,6},{6,2},{1... | collective-permute-start | bytes 393224 | tf_op jit(solution)/shard_map/ppermute | solution.py:156
  18.4 4.3 %collective-permute-start.3 = (bf16[2,32,1024]{2,1,0:T(8,128)(2,1)S(1)}, bf16[2,32,1024]{2,1,0:T(8,128)(2,1)S(1)}, u32[]{:S(2)}, u32[]{:S(2)}) collective-permute-start(bf16[2,32,1024]{2,1,0:T(8,128)(2,1)S(1)} %get-tuple-element.28), channel_id=1, source_target_pairs={{0,4},{4,0},{8,12},{12,8},{1,5},{5,1},{9,13},{13,9},{2,6},{6,2},{1... | collective-permute-start | bytes 393224 | tf_op jit(solution)/shard_map/ppermute | solution.py:156
  19.0 6.4 %collective-permute-start.13 = (bf16[2,32,1024]{2,1,0:T(8,128)(2,1)S(1)}, bf16[2,32,1024]{2,1,0:T(8,128)(2,1)S(1)}, u32[]{:S(2)}, u32[]{:S(2)}) collective-permute-start(bf16[2,32,1024]{2,1,0:T(8,128)(2,1)S(1)} %get-tuple-element.42), channel_id=1, source_target_pairs={{0,8},{4,12},{8,0},{12,4},{1,9},{5,13},{9,1},{13,5},{2,10},{6,14},... | collective-permute-start | bytes 393224 | tf_op jit(solution)/shard_map/ppermute | solution.py:156
  20.6 7.6 %collective-permute-start.10 = (bf16[2,32,1024]{2,1,0:T(8,128)(2,1)S(1)}, bf16[2,32,1024]{2,1,0:T(8,128)(2,1)S(1)}, u32[]{:S(2)}, u32[]{:S(2)}) collective-permute-start(bf16[2,32,1024]{2,1,0:T(8,128)(2,1)S(1)} %get-tuple-element.38), channel_id=1, source_target_pairs={{0,8},{4,12},{8,0},{12,4},{1,9},{5,13},{9,1},{13,5},{2,10},{6,14},... | collective-permute-start | bytes 393224 | tf_op jit(solution)/shard_map/ppermute | solution.py:156
  21.2 9.8 %collective-permute-start.7 = (bf16[2,32,1024]{2,1,0:T(8,128)(2,1)S(1)}, bf16[2,32,1024]{2,1,0:T(8,128)(2,1)S(1)}, u32[]{:S(2)}, u32[]{:S(2)}) collective-permute-start(bf16[2,32,1024]{2,1,0:T(8,128)(2,1)S(1)} %get-tuple-element.34), channel_id=1, source_target_pairs={{0,8},{4,12},{8,0},{12,4},{1,9},{5,13},{9,1},{13,5},{2,10},{6,14},... | collective-permute-start | bytes 393224 | tf_op jit(solution)/shard_map/ppermute | solution.py:156
  22.8 10.1 %collective-permute-start.4 = (bf16[2,32,1024]{2,1,0:T(8,128)(2,1)S(1)}, bf16[2,32,1024]{2,1,0:T(8,128)(2,1)S(1)}, u32[]{:S(2)}, u32[]{:S(2)}) collective-permute-start(bf16[2,32,1024]{2,1,0:T(8,128)(2,1)S(1)} %get-tuple-element.30), channel_id=1, source_target_pairs={{0,8},{4,12},{8,0},{12,4},{1,9},{5,13},{9,1},{13,5},{2,10},{6,14},... | collective-permute-start | bytes 393224 | tf_op jit(solution)/shard_map/ppermute | solution.py:156
  25.5 7.6 %collective-permute-start.14 = (bf16[32,1024]{1,0:T(8,128)(2,1)S(1)}, bf16[32,1024]{1,0:T(8,128)(2,1)S(1)}, u32[]{:S(2)}, u32[]{:S(2)}) collective-permute-start(bf16[32,1024]{1,0:T(8,128)(2,1)S(1)} %shard_map.76.mine_ref), channel_id=1, source_target_pairs={{0,4},{4,0},{8,12},{12,8},{1,5},{5,1},{9,13},{13,9},{2,6},{6,2},{1... | collective-permute-start | bytes 196616 | tf_op jit(solution)/shard_map/ppermute | solution.py:156
  28.3 5.5 %collective-permute-start.11 = (bf16[32,1024]{1,0:T(8,128)(2,1)S(1)}, bf16[32,1024]{1,0:T(8,128)(2,1)S(1)}, u32[]{:S(2)}, u32[]{:S(2)}) collective-permute-start(bf16[32,1024]{1,0:T(8,128)(2,1)S(1)} %shard_map.74.mine_ref), channel_id=1, source_target_pairs={{0,4},{4,0},{8,12},{12,8},{1,5},{5,1},{9,13},{13,9},{2,6},{6,2},{1... | collective-permute-start | bytes 196616 | tf_op jit(solution)/shard_map/ppermute | solution.py:156
  31.1 3.4 %collective-permute-start.8 = (bf16[32,1024]{1,0:T(8,128)(2,1)S(1)}, bf16[32,1024]{1,0:T(8,128)(2,1)S(1)}, u32[]{:S(2)}, u32[]{:S(2)}) collective-permute-start(bf16[32,1024]{1,0:T(8,128)(2,1)S(1)} %shard_map.71.mine_ref), channel_id=1, source_target_pairs={{0,4},{4,0},{8,12},{12,8},{1,5},{5,1},{9,13},{13,9},{2,6},{6,2},{1... | collective-permute-start | bytes 196616 | tf_op jit(solution)/shard_map/ppermute | solution.py:156
  33.0 2.2 %collective-permute-start.5 = (bf16[32,1024]{1,0:T(8,128)(2,1)S(1)}, bf16[32,1024]{1,0:T(8,128)(2,1)S(1)}, u32[]{:S(2)}, u32[]{:S(2)}) collective-permute-start(bf16[32,1024]{1,0:T(8,128)(2,1)S(1)} %shard_map.68.mine_ref), channel_id=1, source_target_pairs={{0,4},{4,0},{8,12},{12,8},{1,5},{5,1},{9,13},{13,9},{2,6},{6,2},{1... | collective-permute-start | bytes 196616 | tf_op jit(solution)/shard_map/ppermute | solution.py:156
  34.5 9.2 %copy-start.2 = (s32[32,2]{0,1:T(2,128)S(1)}, s32[32,2]{0,1:T(2,128)}, u32[]{:S(2)}) copy-start(s32[32,2]{0,1:T(2,128)} %param.10) | copy-start | bytes 772
  34.5 9.2 %copy-start.3 = (f32[32,2]{0,1:T(2,128)S(1)}, f32[32,2]{0,1:T(2,128)}, u32[]{:S(2)}) copy-start(f32[32,2]{0,1:T(2,128)} %param.11) | copy-start | bytes 772
  35.9 4.5 %collective-permute-start.15 = (bf16[16,1536]{1,0:T(8,128)(2,1)S(1)}, bf16[16,1536]{1,0:T(8,128)(2,1)S(1)}, u32[]{:S(2)}, u32[]{:S(2)}) collective-permute-start(bf16[16,1536]{1,0:T(8,128)(2,1)S(1)} %get-tuple-element.44), channel_id=1, source_target_pairs={{0,1},{1,0},{2,3},{3,2},{4,5},{5,4},{6,7},{7,6},{8,9},{9,8},{10,11... | collective-permute-start | bytes 147464 | tf_op jit(solution)/shard_map/ppermute | solution.py:156
  36.0 7.7 %collective-permute-start.16 = (bf16[16,1536]{1,0:T(8,128)(2,1)S(1)}, bf16[16,1536]{1,0:T(8,128)(2,1)S(1)}, u32[]{:S(2)}, u32[]{:S(2)}) collective-permute-start(bf16[16,1536]{1,0:T(8,128)(2,1)S(1)} %get-tuple-element.45), channel_id=1, source_target_pairs={{0,2},{1,3},{2,0},{3,1},{4,6},{5,7},{6,4},{7,5},{8,10},{9,11},{10,... | collective-permute-start | bytes 147464 | tf_op jit(solution)/shard_map/ppermute | solution.py:156
  37.3 6.4 %collective-permute-start.17 = (bf16[16,1536]{1,0:T(8,128)(2,1)S(1)}, bf16[16,1536]{1,0:T(8,128)(2,1)S(1)}, u32[]{:S(2)}, u32[]{:S(2)}) collective-permute-start(bf16[16,1536]{1,0:T(8,128)(2,1)S(1)} %get-tuple-element.46), channel_id=1, source_target_pairs={{0,3},{1,2},{2,1},{3,0},{4,7},{5,6},{6,5},{7,4},{8,11},{9,10},{10,... | collective-permute-start | bytes 147464 | tf_op jit(solution)/shard_map/ppermute | solution.py:156
where the time goes:
time: 44.7 us; the launch traced here: 44.5 us
  waiting for transfers between devices  18.3 us (41%)
  starting transfers between devices  16 us (36%)
  Pallas kernels  9.98 us (22%)
    ppermute x18, waiting for transfers between devices, swap(): return lax.ppermute(value, axis, [(i, i ^ mask) for i in range(size)])  18.3 us
    ppermute x18, starting transfers between devices, swap(): return lax.ppermute(value, axis, [(i, i ^ mask) for i in range(size)])  16 us
    pallas_call x18, Pallas kernels, call(): pl.pallas_call(body, out_shape=outs, in_specs=[spec] * len(args), out_spe...  9.98 us
  transfers between devices with their start and end apart: 18, of which 7 were waited for; matrix products, arithmetic and copies ran while one was open for 0% of the time, Pallas kernels for 13%

commit v1 on v0

--- a/solution.py
+++ b/solution.py
@@ -13,17 +13,18 @@
 BF16 = jnp.bfloat16
 PRIOR = 100000
 WIDE = 2048
+PIECES = 2
 CUTS = (0, 4, 8, 12, 16)
 GRANT = 2 * 1024 * 1024
 VM = pl.BlockSpec(memory_space=pltpu.VMEM)
 
 
-def call(body, outs, flops, nbytes, *args, scratch=(), spec=VM):
+def call(body, outs, flops, nbytes, *args, scratch=(), spec=VM, out_spec=VM):
     return pl.pallas_call(
         body,
         out_shape=outs,
         in_specs=[spec] * len(args),
-        out_specs=jax.tree.map(lambda _: VM, outs),
+        out_specs=jax.tree.map(lambda _: out_spec, outs),
         scratch_shapes=scratch,
         compiler_params=pltpu.CompilerParams(vmem_limit_bytes=GRANT),
         cost_estimate=pl.CostEstimate(flops=flops, bytes_accessed=nbytes, transcendentals=0),
@@ -54,16 +55,28 @@
     return jnp.where((slot == rank) & (routed > 0.0), 1.0, 0.0).astype(BF16)
 
 
-def pack_body(ids_hbm, tokens_hbm, out_ref, ids_ref, tokens_ref, sems):
+def pack_body(ids_hbm, routes_hbm, tokens_hbm, out_ref, slots_ref, combine_ref, ids_ref, routes_ref, tokens_ref, sems):
     copies = [
-        pltpu.make_async_copy(ids_hbm, ids_ref, sems.at[0]),
-        pltpu.make_async_copy(tokens_hbm, tokens_ref, sems.at[1]),
+        pltpu.make_async_copy(source, target, sems.at[i])
+        for i, (source, target) in enumerate(
+            ((tokens_hbm, tokens_ref), (ids_hbm, ids_ref), (routes_hbm, routes_ref))
+        )
     ]
     for copy in copies:
         copy.start()
+    copies[1].wait()
+    copies[2].wait()
+    ids = ids_ref[...]
+    count = ids.shape[1]
+    slots_ref[...] = slots(ids, slots_ref.shape[1])
+    held = jnp.sum(jnp.where(ids == 0, routes_ref[...], 0.0), axis=0, keepdims=True)
+    row = lax.broadcasted_iota(jnp.int32, (count, count), 0)
+    col = lax.broadcasted_iota(jnp.int32, (count, count), 1)
+    combine_ref[...] = jnp.sum(
+        jnp.where(col == row, jnp.broadcast_to(held, (count, count)), 0.0), axis=1, keepdims=True
+    )
+    one_hot = slots(ids, MOST)
     copies[0].wait()
-    one_hot = slots(ids_ref[...], MOST)
-    copies[1].wait()
     out_ref[...] = lax.dot_general(
         one_hot, tokens_ref[...], (((0,), (0,)), ((), ())), preferred_element_type=F32
     ).astype(BF16)
@@ -132,24 +145,24 @@
             sends[q - 1][...] = block.astype(BF16)
 
 
-def final_body(ids_ref, route_ref, own_ref, *refs):
-    out_ref = refs[-1]
-    own = own_ref[...]
-    high = own.astype(BF16)
-    rest = own - high.astype(F32)
-    mid = rest.astype(BF16)
-    low = (rest - mid.astype(F32)).astype(BF16)
-    terms = jnp.concatenate([high, mid, low] + [got[...] for got in refs[:-1]], axis=0)
-    ids = ids_ref[...]
-    count = ids.shape[1]
-    held = jnp.sum(jnp.where(ids == 0, route_ref[...], 0.0), axis=0, keepdims=True)
-    row = lax.broadcasted_iota(jnp.int32, (count, count), 0)
-    col = lax.broadcasted_iota(jnp.int32, (count, count), 1)
-    combine = jnp.sum(
-        jnp.where(col == row, jnp.broadcast_to(held, (count, count)), 0.0), axis=1, keepdims=True
-    )
-    spread = jnp.dot(slots(ids, terms.shape[0]), terms, preferred_element_type=F32)
-    out_ref[...] = (combine * spread).astype(BF16)
+def final_body(slots_ref, combine_ref, own_ref, *refs):
+    *gots, out_hbm, out_ref, sems = refs
+    width = out_ref.shape[1] // PIECES
+    copies = []
+    for i in range(PIECES):
+        at = slice(i * width, (i + 1) * width)
+        own = own_ref[:, at]
+        high = own.astype(BF16)
+        rest = own - high.astype(F32)
+        mid = rest.astype(BF16)
+        low = (rest - mid.astype(F32)).astype(BF16)
+        terms = jnp.concatenate([high, mid, low] + [got[:, at] for got in gots], axis=0)
+        spread = jnp.dot(slots_ref[...], terms, preferred_element_type=F32)
+        out_ref[:, at] = (combine_ref[...] * spread).astype(BF16)
+        copies.append(pltpu.make_async_copy(out_ref.at[:, at], out_hbm.at[:, at], sems.at[i]))
+        copies[i].start()
+    for copy in copies:
+        copy.wait()
 
 
 def swap(value, axis, size, mask):
@@ -162,17 +175,20 @@
     out_width = down_weight.shape[1]
     total = MOST * n_tp
     gate_weight, up_weight, down_weight = map(in_vmem, (gate_weight, up_weight, down_weight))
-    packed = call(
+    count = tokens.shape[0]
+    packed, spot, combine = call(
         pack_body,
-        shape((MOST, model), BF16),
+        [shape((MOST, model), BF16), shape((count, (n_tp + 2) * MOST), BF16), shape((count, 1), F32)],
         PRIOR * total * model * width,
         PRIOR * model * width,
         in_hbm(ids_t),
+        in_hbm(route_t),
         in_hbm(tokens),
         scratch=[
             pltpu.VMEM(ids_t.shape, ids_t.dtype),
+            pltpu.VMEM(route_t.shape, route_t.dtype),
             pltpu.VMEM(tokens.shape, tokens.dtype),
-            pltpu.SemaphoreType.DMA((2,)),
+            pltpu.SemaphoreType.DMA((3,)),
         ],
         spec=pl.BlockSpec(memory_space=pltpu.HBM),
     )
@@ -233,9 +249,18 @@
     got = []
     for q, send in enumerate(sends):
         got.append(swap(send, "tp", n_tp, q + 1))
+    dims = (count, out_width)
     return call(
-        final_body, shape((tokens.shape[0], out_width), BF16), 2 * tokens.size, 4 * tokens.size,
-        ids_t, route_t, own, *got,
+        final_body,
+        shape(dims, BF16),
+        2 * tokens.size,
+        4 * tokens.size,
+        spot,
+        combine,
+        own,
+        *got,
+        scratch=[pltpu.VMEM(dims, BF16), pltpu.SemaphoreType.DMA((PIECES,))],
+        out_spec=pl.BlockSpec(memory_space=pltpu.HBM),
     )
 
 

time: 44.7 us -> 44.6 us (level)
  no operation moved by 1% of the time
where the time goes in v1:
time: 44.6 us; the launch traced here: 44.4 us
  waiting for transfers between devices  18.3 us (41%)
  starting transfers between devices  16 us (36%)
  Pallas kernels  9.9 us (22%)
    ppermute x18, waiting for transfers between devices, swap(): return lax.ppermute(value, axis, [(i, i ^ mask) for i in range(size)])  18.3 us
    ppermute x18, starting transfers between devices, swap(): return lax.ppermute(value, axis, [(i, i ^ mask) for i in range(size)])  16 us
    pallas_call x18, Pallas kernels, call(): pl.pallas_call(body, out_shape=outs, in_specs=[spec] * len(args), out_spe...  9.9 us
  transfers between devices with their start and end apart: 18, of which 7 were waited for; matrix products, arithmetic and copies ran while one was open for 0% of the time, Pallas kernels for 13%

profile of v1, /device:TPU:0, one launch (start us, length us, event | category | flops | bytes accessed | tf_op | source)
XLA Modules:
  0.0 44.4 jit_solution(3612996350948466787)
XLA Ops:
  0.0 1.2 %shard_map.64 = (bf16[16,1536]{1,0:T(8,128)(2,1)S(1)}, bf16[32,96]{1,0:T(8,128)(2,1)S(1)}, f32[32,1]{1,0:T(8,128)S(1)}) custom-call(s32[2,32]{1,0:T(2,128)} %bitcast.4, f32[2,32]{1,0:T(2,128)} %bitcast.5, bf16[32,1536]{1,0:T(8,128)(2,1)} %tokens_hbm.1), custom_call_target="tpu_custom_call" | custom-call | flops 40265318400000 | bytes 629145600000 | tf_op jit(solution)/shard_map/pallas_call | solution.py:23
  1.3 3.1 %collective-permute-start = (bf16[16,1536]{1,0:T(8,128)(2,1)S(1)}, bf16[16,1536]{1,0:T(8,128)(2,1)S(1)}, u32[]{:S(2)}, u32[]{:S(2)}) collective-permute-start(bf16[16,1536]{1,0:T(8,128)(2,1)S(1)} %get-tuple-element.31.refs_0_), channel_id=1, source_target_pairs={{0,1},{1,0},{2,3},{3,2},{4,5},{5,4},{6,7},{7,6},{8,9},{9,8},{10,11... | collective-permute-start | bytes 147464 | tf_op jit(solution)/shard_map/ppermute | solution.py:169
  4.4 2.6 %collective-permute-start.1 = (bf16[16,1536]{1,0:T(8,128)(2,1)S(1)}, bf16[16,1536]{1,0:T(8,128)(2,1)S(1)}, u32[]{:S(2)}, u32[]{:S(2)}) collective-permute-start(bf16[16,1536]{1,0:T(8,128)(2,1)S(1)} %get-tuple-element.31.refs_0_), channel_id=1, source_target_pairs={{0,2},{1,3},{2,0},{3,1},{4,6},{5,7},{6,4},{7,5},{8,10},{9,11},{10,... | collective-permute-start | bytes 147464 | tf_op jit(solution)/shard_map/ppermute | solution.py:169
  7.0 0.0 collective-permute-start.2
  7.0 0.0 collective-permute-done.refs_1_
  7.0 3.3 %collective-permute-done.1.refs_2_ = bf16[16,1536]{1,0:T(8,128)(2,1)S(1)} collective-permute-done((bf16[16,1536]{1,0:T(8,128)(2,1)S(1)}, bf16[16,1536]{1,0:T(8,128)(2,1)S(1)}, u32[]{:S(2)}, u32[]{:S(2)}) %collective-permute-start.1) | collective-permute-done | bytes 49184 | tf_op jit(solution)/shard_map/ppermute | solution.py:169
  10.3 2.6 %collective-permute-done.2.refs_3_ = bf16[16,1536]{1,0:T(8,128)(2,1)S(1)} collective-permute-done((bf16[16,1536]{1,0:T(8,128)(2,1)S(1)}, bf16[16,1536]{1,0:T(8,128)(2,1)S(1)}, u32[]{:S(2)}, u32[]{:S(2)}) %collective-permute-start.2) | collective-permute-done | bytes 49184 | tf_op jit(solution)/shard_map/ppermute | solution.py:169
  12.9 1.2 %shard_map.65 = (bf16[2,32,1024]{2,1,0:T(8,128)(2,1)S(1)}, bf16[2,32,1024]{2,1,0:T(8,128)(2,1)S(1)}, bf16[64,1536]{1,0:T(8,128)(2,1)S(1)}) custom-call(bf16[16,1536]{1,0:T(8,128)(2,1)S(1)} %get-tuple-element.31.refs_0_, bf16[16,1536]{1,0:T(8,128)(2,1)S(1)} %collective-permute-done.refs_1_, bf16[16,1536]{1,0:T(8,128)(2,1)S(1)} %collective-permute-done.1.refs_2_, ...), custom_call_target="tpu_custom_call" | custom-call | flops 402653184 | bytes 6291456 | tf_op jit(solution)/shard_map/pallas_call | solution.py:23
  14.1 0.1 collective-permute-start.12
  14.1 1.2 %shard_map.72 = (bf16[2,32,1024]{2,1,0:T(8,128)(2,1)S(1)}, bf16[2,32,1024]{2,1,0:T(8,128)(2,1)S(1)}) custom-call(bf16[64,1536]{1,0:T(8,128)(2,1)S(1)} %get-tuple-element.32.rows_ref, bf16[1536,4096]{1,0:T(8,128)(2,1)S(1)} %copy-done, bf16[1536,4096]{1,0:T(8,128)(2,1)S(1)} %copy-done.1), custom_call_target="tpu_custom_call" | custom-call | flops 402653184 | bytes 6291456 | tf_op jit(solution)/shard_map/pallas_call | solution.py:23
  15.4 0.0 slice-start
  15.4 0.0 slice-start.1
  15.4 1.2 %shard_map.69 = (bf16[2,32,1024]{2,1,0:T(8,128)(2,1)S(1)}, bf16[2,32,1024]{2,1,0:T(8,128)(2,1)S(1)}) custom-call(bf16[64,1536]{1,0:T(8,128)(2,1)S(1)} %get-tuple-element.32.rows_ref, bf16[1536,4096]{1,0:T(8,128)(2,1)S(1)} %copy-done, bf16[1536,4096]{1,0:T(8,128)(2,1)S(1)} %copy-done.1), custom_call_target="tpu_custom_call" | custom-call | flops 402653184 | bytes 6291456 | tf_op jit(solution)/shard_map/pallas_call | solution.py:23
  16.6 0.0 slice-start.2
  16.6 0.6 %collective-permute-start.9 = (bf16[2,32,1024]{2,1,0:T(8,128)(2,1)S(1)}, bf16[2,32,1024]{2,1,0:T(8,128)(2,1)S(1)}, u32[]{:S(2)}, u32[]{:S(2)}) collective-permute-start(bf16[2,32,1024]{2,1,0:T(8,128)(2,1)S(1)} %get-tuple-element.42), channel_id=1, source_target_pairs={{0,4},{4,0},{8,12},{12,8},{1,5},{5,1},{9,13},{13,9},{2,6},{6,2},{1... | collective-permute-start | bytes 393224 | tf_op jit(solution)/shard_map/ppermute | solution.py:169
  17.2 0.1 collective-permute-start.6
  17.2 1.2 %shard_map.66 = (bf16[2,32,1024]{2,1,0:T(8,128)(2,1)S(1)}, bf16[2,32,1024]{2,1,0:T(8,128)(2,1)S(1)}) custom-call(bf16[64,1536]{1,0:T(8,128)(2,1)S(1)} %get-tuple-element.32.rows_ref, bf16[1536,4096]{1,0:T(8,128)(2,1)S(1)} %copy-done, bf16[1536,4096]{1,0:T(8,128)(2,1)S(1)} %copy-done.1), custom_call_target="tpu_custom_call" | custom-call | flops 402653184 | bytes 6291456 | tf_op jit(solution)/shard_map/pallas_call | solution.py:23
  18.4 0.5 %collective-permute-start.3 = (bf16[2,32,1024]{2,1,0:T(8,128)(2,1)S(1)}, bf16[2,32,1024]{2,1,0:T(8,128)(2,1)S(1)}, u32[]{:S(2)}, u32[]{:S(2)}) collective-permute-start(bf16[2,32,1024]{2,1,0:T(8,128)(2,1)S(1)} %get-tuple-element.34), channel_id=1, source_target_pairs={{0,4},{4,0},{8,12},{12,8},{1,5},{5,1},{9,13},{13,9},{2,6},{6,2},{1... | collective-permute-start | bytes 393224 | tf_op jit(solution)/shard_map/ppermute | solution.py:169
  18.9 0.0 collective-permute-done.12.got_ref
  19.0 1.6 %collective-permute-start.13 = (bf16[2,32,1024]{2,1,0:T(8,128)(2,1)S(1)}, bf16[2,32,1024]{2,1,0:T(8,128)(2,1)S(1)}, u32[]{:S(2)}, u32[]{:S(2)}) collective-permute-start(bf16[2,32,1024]{2,1,0:T(8,128)(2,1)S(1)} %get-tuple-element.48), channel_id=1, source_target_pairs={{0,8},{4,12},{8,0},{12,4},{1,9},{5,13},{9,1},{13,5},{2,10},{6,14},... | collective-permute-start | bytes 393224 | tf_op jit(solution)/shard_map/ppermute | solution.py:169
  20.6 0.6 %collective-permute-start.10 = (bf16[2,32,1024]{2,1,0:T(8,128)(2,1)S(1)}, bf16[2,32,1024]{2,1,0:T(8,128)(2,1)S(1)}, u32[]{:S(2)}, u32[]{:S(2)}) collective-permute-start(bf16[2,32,1024]{2,1,0:T(8,128)(2,1)S(1)} %get-tuple-element.44), channel_id=1, source_target_pairs={{0,8},{4,12},{8,0},{12,4},{1,9},{5,13},{9,1},{13,5},{2,10},{6,14},... | collective-permute-start | bytes 393224 | tf_op jit(solution)/shard_map/ppermute | solution.py:169
  21.2 0.0 collective-permute-done.6.got_ref
  21.2 1.6 %collective-permute-start.7 = (bf16[2,32,1024]{2,1,0:T(8,128)(2,1)S(1)}, bf16[2,32,1024]{2,1,0:T(8,128)(2,1)S(1)}, u32[]{:S(2)}, u32[]{:S(2)}) collective-permute-start(bf16[2,32,1024]{2,1,0:T(8,128)(2,1)S(1)} %get-tuple-element.40), channel_id=1, source_target_pairs={{0,8},{4,12},{8,0},{12,4},{1,9},{5,13},{9,1},{13,5},{2,10},{6,14},... | collective-permute-start | bytes 393224 | tf_op jit(solution)/shard_map/ppermute | solution.py:169
  22.8 0.6 %collective-permute-start.4 = (bf16[2,32,1024]{2,1,0:T(8,128)(2,1)S(1)}, bf16[2,32,1024]{2,1,0:T(8,128)(2,1)S(1)}, u32[]{:S(2)}, u32[]{:S(2)}) collective-permute-start(bf16[2,32,1024]{2,1,0:T(8,128)(2,1)S(1)} %get-tuple-element.36), channel_id=1, source_target_pairs={{0,8},{4,12},{8,0},{12,4},{1,9},{5,13},{9,1},{13,5},{2,10},{6,14},... | collective-permute-start | bytes 393224 | tf_op jit(solution)/shard_map/ppermute | solution.py:169
  23.4 2.0 %collective-permute-done.13.got_ref = bf16[2,32,1024]{2,1,0:T(8,128)(2,1)S(1)} collective-permute-done((bf16[2,32,1024]{2,1,0:T(8,128)(2,1)S(1)}, bf16[2,32,1024]{2,1,0:T(8,128)(2,1)S(1)}, u32[]{:S(2)}, u32[]{:S(2)}) %collective-permute-start.13) | collective-permute-done | bytes 131104 | tf_op jit(solution)/shard_map/ppermute | solution.py:169
  25.4 0.1 shard_map.76.mine_ref
  25.5 0.1 collective-permute-start.14
  25.6 2.7 %collective-permute-done.10.got_ref = bf16[2,32,1024]{2,1,0:T(8,128)(2,1)S(1)} collective-permute-done((bf16[2,32,1024]{2,1,0:T(8,128)(2,1)S(1)}, bf16[2,32,1024]{2,1,0:T(8,128)(2,1)S(1)}, u32[]{:S(2)}, u32[]{:S(2)}) %collective-permute-start.10) | collective-permute-done | bytes 131104 | tf_op jit(solution)/shard_map/ppermute | solution.py:169
  28.2 0.1 shard_map.74.mine_ref
  28.3 0.1 collective-permute-start.11
  28.4 2.7 %collective-permute-done.7.got_ref = bf16[2,32,1024]{2,1,0:T(8,128)(2,1)S(1)} collective-permute-done((bf16[2,32,1024]{2,1,0:T(8,128)(2,1)S(1)}, bf16[2,32,1024]{2,1,0:T(8,128)(2,1)S(1)}, u32[]{:S(2)}, u32[]{:S(2)}) %collective-permute-start.7) | collective-permute-done | bytes 131104 | tf_op jit(solution)/shard_map/ppermute | solution.py:169
  31.0 0.1 shard_map.71.mine_ref
  31.1 0.1 collective-permute-start.8
  31.2 1.8 %collective-permute-done.4.got_ref = bf16[2,32,1024]{2,1,0:T(8,128)(2,1)S(1)} collective-permute-done((bf16[2,32,1024]{2,1,0:T(8,128)(2,1)S(1)}, bf16[2,32,1024]{2,1,0:T(8,128)(2,1)S(1)}, u32[]{:S(2)}, u32[]{:S(2)}) %collective-permute-start.4) | collective-permute-done | bytes 131104 | tf_op jit(solution)/shard_map/ppermute | solution.py:169
  33.0 0.1 shard_map.68.mine_ref
  33.0 0.1 collective-permute-start.5
  33.1 0.0 collective-permute-done.14.beside_ref
  33.1 0.6 %shard_map.77.refs_0_ = f32[64,1536]{1,0:T(8,128)S(1)} custom-call(bf16[32,1024]{1,0:T(8,128)(2,1)S(1)} %shard_map.76.mine_ref, bf16[32,1024]{1,0:T(8,128)(2,1)S(1)} %collective-permute-done.14.beside_ref, bf16[4096,1536]{1,0:T(8,128)(2,1)S(1)} %bitcast.3), custom_call_target="tpu_custom_call" | custom-call | flops 201326592 | bytes 3145728 | tf_op jit(solution)/shard_map/pallas_call | solution.py:23
  33.8 0.0 collective-permute-done.11.beside_ref
  33.8 0.7 %shard_map.78.refs_0_ = f32[64,1536]{1,0:T(8,128)S(1)} custom-call(bf16[32,1024]{1,0:T(8,128)(2,1)S(1)} %shard_map.74.mine_ref, bf16[32,1024]{1,0:T(8,128)(2,1)S(1)} %collective-permute-done.11.beside_ref, bf16[4096,1536]{1,0:T(8,128)(2,1)S(1)} %bitcast.3, f32[64,1536]{1,0:T(8,128)S(1)} %shard_map.77.refs_0_), custom_call_target="tpu_custom_call" | custom-call | flops 201326592 | bytes 3145728 | tf_op jit(solution)/shard_map/pallas_call | solution.py:23
  34.5 0.7 %shard_map.79.total_ref = f32[64,1536]{1,0:T(8,128)S(1)} custom-call(bf16[32,1024]{1,0:T(8,128)(2,1)S(1)} %shard_map.71.mine_ref, bf16[32,1024]{1,0:T(8,128)(2,1)S(1)} %collective-permute-done.8.beside_ref, bf16[4096,1536]{1,0:T(8,128)(2,1)S(1)} %bitcast.3, f32[64,1536]{1,0:T(8,128)S(1)} %shard_map.78.refs_0_), custom_call_target="tpu_custom_call" | custom-call | flops 201326592 | bytes 3145728 | tf_op jit(solution)/shard_map/pallas_call | solution.py:23
  35.2 0.0 collective-permute-done.5.beside_ref
  35.2 0.7 %shard_map.80 = (f32[16,1536]{1,0:T(8,128)S(1)}, bf16[16,1536]{1,0:T(8,128)(2,1)S(1)}, bf16[16,1536]{1,0:T(8,128)(2,1)S(1)}, bf16[16,1536]{1,0:T(8,128)(2,1)S(1)}) custom-call(bf16[32,1024]{1,0:T(8,128)(2,1)S(1)} %shard_map.68.mine_ref, bf16[32,1024]{1,0:T(8,128)(2,1)S(1)} %collective-permute-done.5.beside_ref, bf16[4096,1536]{1,0:T(8,128)(2,1)S(1)} %bitcast.3, ...), custom_call_target="tpu_custom_call" | custom-call | flops 201326592 | bytes 3145728 | tf_op jit(solution)/shard_map/pallas_call | solution.py:23
  35.9 0.1 collective-permute-start.15
  35.9 1.3 %collective-permute-start.16 = (bf16[16,1536]{1,0:T(8,128)(2,1)S(1)}, bf16[16,1536]{1,0:T(8,128)(2,1)S(1)}, u32[]{:S(2)}, u32[]{:S(2)}) collective-permute-start(bf16[16,1536]{1,0:T(8,128)(2,1)S(1)} %get-tuple-element.51), channel_id=1, source_target_pairs={{0,2},{1,3},{2,0},{3,1},{4,6},{5,7},{6,4},{7,5},{8,10},{9,11},{10,... | collective-permute-start | bytes 147464 | tf_op jit(solution)/shard_map/ppermute | solution.py:169
  37.2 3.1 %collective-permute-start.17 = (bf16[16,1536]{1,0:T(8,128)(2,1)S(1)}, bf16[16,1536]{1,0:T(8,128)(2,1)S(1)}, u32[]{:S(2)}, u32[]{:S(2)}) collective-permute-start(bf16[16,1536]{1,0:T(8,128)(2,1)S(1)} %get-tuple-element.52), channel_id=1, source_target_pairs={{0,3},{1,2},{2,1},{3,0},{4,7},{5,6},{6,5},{7,4},{8,11},{9,10},{10,... | collective-permute-start | bytes 147464 | tf_op jit(solution)/shard_map/ppermute | solution.py:169
  40.3 3.3 %collective-permute-done.16.refs_1_ = bf16[16,1536]{1,0:T(8,128)(2,1)S(1)} collective-permute-done((bf16[16,1536]{1,0:T(8,128)(2,1)S(1)}, bf16[16,1536]{1,0:T(8,128)(2,1)S(1)}, u32[]{:S(2)}, u32[]{:S(2)}) %collective-permute-start.16) | collective-permute-done | bytes 49184 | tf_op jit(solution)/shard_map/ppermute | solution.py:169
  43.6 0.8 %shard_map.81 = bf16[32,1536]{1,0:T(8,128)(2,1)} custom-call(bf16[32,96]{1,0:T(8,128)(2,1)S(1)} %get-tuple-element.29.slots_ref, f32[32,1]{1,0:T(8,128)S(1)} %get-tuple-element.30.combine_ref, f32[16,1536]{1,0:T(8,128)S(1)} %get-tuple-element.49.own_ref, bf16[16,1536]{1,0:T(8,128)(2,1)S(1)} %collective-permute-done.15.refs_0_, ...), custom_call_target="tpu_custom_call" | custom-call | flops 98304 | bytes 196608 | tf_op jit(solution)/shard_map/pallas_call | solution.py:23
  (17 shorter events, 0.2 us)
Async XLA Ops:
  0.0 12.9 %copy-start = (bf16[1536,4096]{1,0:T(8,128)(2,1)S(1)}, bf16[1536,4096]{1,0:T(8,128)(2,1)}, u32[]{:S(2)}) copy-start(bf16[1536,4096]{1,0:T(8,128)(2,1)} %gate_ref.5) | copy-start | bytes 37748740
  0.0 12.9 %copy-start.1 = (bf16[1536,4096]{1,0:T(8,128)(2,1)S(1)}, bf16[1536,4096]{1,0:T(8,128)(2,1)}, u32[]{:S(2)}) copy-start(bf16[1536,4096]{1,0:T(8,128)(2,1)} %up_ref.5) | copy-start | bytes 37748740
  1.3 5.7 %collective-permute-start = (bf16[16,1536]{1,0:T(8,128)(2,1)S(1)}, bf16[16,1536]{1,0:T(8,128)(2,1)S(1)}, u32[]{:S(2)}, u32[]{:S(2)}) collective-permute-start(bf16[16,1536]{1,0:T(8,128)(2,1)S(1)} %get-tuple-element.31.refs_0_), channel_id=1, source_target_pairs={{0,1},{1,0},{2,3},{3,2},{4,5},{5,4},{6,7},{7,6},{8,9},{9,8},{10,11... | collective-permute-start | bytes 147464 | tf_op jit(solution)/shard_map/ppermute | solution.py:169
  4.4 5.9 %collective-permute-start.1 = (bf16[16,1536]{1,0:T(8,128)(2,1)S(1)}, bf16[16,1536]{1,0:T(8,128)(2,1)S(1)}, u32[]{:S(2)}, u32[]{:S(2)}) collective-permute-start(bf16[16,1536]{1,0:T(8,128)(2,1)S(1)} %get-tuple-element.31.refs_0_), channel_id=1, source_target_pairs={{0,2},{1,3},{2,0},{3,1},{4,6},{5,7},{6,4},{7,5},{8,10},{9,11},{10,... | collective-permute-start | bytes 147464 | tf_op jit(solution)/shard_map/ppermute | solution.py:169
  7.0 5.9 %collective-permute-start.2 = (bf16[16,1536]{1,0:T(8,128)(2,1)S(1)}, bf16[16,1536]{1,0:T(8,128)(2,1)S(1)}, u32[]{:S(2)}, u32[]{:S(2)}) collective-permute-start(bf16[16,1536]{1,0:T(8,128)(2,1)S(1)} %get-tuple-element.31.refs_0_), channel_id=1, source_target_pairs={{0,3},{1,2},{2,1},{3,0},{4,7},{5,6},{6,5},{7,4},{8,11},{9,10},{10,... | collective-permute-start | bytes 147464 | tf_op jit(solution)/shard_map/ppermute | solution.py:169
  14.1 4.9 %collective-permute-start.12 = (bf16[2,32,1024]{2,1,0:T(8,128)(2,1)S(1)}, bf16[2,32,1024]{2,1,0:T(8,128)(2,1)S(1)}, u32[]{:S(2)}, u32[]{:S(2)}) collective-permute-start(bf16[2,32,1024]{2,1,0:T(8,128)(2,1)S(1)} %get-tuple-element.46), channel_id=1, source_target_pairs={{0,4},{4,0},{8,12},{12,8},{1,5},{5,1},{9,13},{13,9},{2,6},{6,2},{1... | collective-permute-start | bytes 393224 | tf_op jit(solution)/shard_map/ppermute | solution.py:169
  15.4 17.8 %slice-start = ((s8[12582912]{0:T(1024)(128)(4,1)}), s8[4194304]{0:T(1024)(128)(4,1)S(1)}, s32[]{:S(2)}) async-start(s8[12582912]{0:T(1024)(128)(4,1)} %bitcast.2), calls=%async_computation | async-start | bytes 8388608
  15.4 17.8 %slice-start.1 = ((s8[12582912]{0:T(1024)(128)(4,1)}), s8[4194304]{0:T(1024)(128)(4,1)S(1)}, s32[]{:S(2)}) async-start(s8[12582912]{0:T(1024)(128)(4,1)} %bitcast.2), calls=%async_computation.1 | async-start | bytes 8388608
  16.6 16.5 %slice-start.2 = ((s8[12582912]{0:T(1024)(128)(4,1)}), s8[4194304]{0:T(1024)(128)(4,1)S(1)}, s32[]{:S(2)}) async-start(s8[12582912]{0:T(1024)(128)(4,1)} %bitcast.2), calls=%async_computation.2 | async-start | bytes 8388608
  16.6 3.9 %collective-permute-start.9 = (bf16[2,32,1024]{2,1,0:T(8,128)(2,1)S(1)}, bf16[2,32,1024]{2,1,0:T(8,128)(2,1)S(1)}, u32[]{:S(2)}, u32[]{:S(2)}) collective-permute-start(bf16[2,32,1024]{2,1,0:T(8,128)(2,1)S(1)} %get-tuple-element.42), channel_id=1, source_target_pairs={{0,4},{4,0},{8,12},{12,8},{1,5},{5,1},{9,13},{13,9},{2,6},{6,2},{1... | collective-permute-start | bytes 393224 | tf_op jit(solution)/shard_map/ppermute | solution.py:169
  17.2 4.0 %collective-permute-start.6 = (bf16[2,32,1024]{2,1,0:T(8,128)(2,1)S(1)}, bf16[2,32,1024]{2,1,0:T(8,128)(2,1)S(1)}, u32[]{:S(2)}, u32[]{:S(2)}) collective-permute-start(bf16[2,32,1024]{2,1,0:T(8,128)(2,1)S(1)} %get-tuple-element.38), channel_id=1, source_target_pairs={{0,4},{4,0},{8,12},{12,8},{1,5},{5,1},{9,13},{13,9},{2,6},{6,2},{1... | collective-permute-start | bytes 393224 | tf_op jit(solution)/shard_map/ppermute | solution.py:169
  18.4 4.4 %collective-permute-start.3 = (bf16[2,32,1024]{2,1,0:T(8,128)(2,1)S(1)}, bf16[2,32,1024]{2,1,0:T(8,128)(2,1)S(1)}, u32[]{:S(2)}, u32[]{:S(2)}) collective-permute-start(bf16[2,32,1024]{2,1,0:T(8,128)(2,1)S(1)} %get-tuple-element.34), channel_id=1, source_target_pairs={{0,4},{4,0},{8,12},{12,8},{1,5},{5,1},{9,13},{13,9},{2,6},{6,2},{1... | collective-permute-start | bytes 393224 | tf_op jit(solution)/shard_map/ppermute | solution.py:169
  19.0 6.4 %collective-permute-start.13 = (bf16[2,32,1024]{2,1,0:T(8,128)(2,1)S(1)}, bf16[2,32,1024]{2,1,0:T(8,128)(2,1)S(1)}, u32[]{:S(2)}, u32[]{:S(2)}) collective-permute-start(bf16[2,32,1024]{2,1,0:T(8,128)(2,1)S(1)} %get-tuple-element.48), channel_id=1, source_target_pairs={{0,8},{4,12},{8,0},{12,4},{1,9},{5,13},{9,1},{13,5},{2,10},{6,14},... | collective-permute-start | bytes 393224 | tf_op jit(solution)/shard_map/ppermute | solution.py:169
  20.6 7.6 %collective-permute-start.10 = (bf16[2,32,1024]{2,1,0:T(8,128)(2,1)S(1)}, bf16[2,32,1024]{2,1,0:T(8,128)(2,1)S(1)}, u32[]{:S(2)}, u32[]{:S(2)}) collective-permute-start(bf16[2,32,1024]{2,1,0:T(8,128)(2,1)S(1)} %get-tuple-element.44), channel_id=1, source_target_pairs={{0,8},{4,12},{8,0},{12,4},{1,9},{5,13},{9,1},{13,5},{2,10},{6,14},... | collective-permute-start | bytes 393224 | tf_op jit(solution)/shard_map/ppermute | solution.py:169
  21.2 9.8 %collective-permute-start.7 = (bf16[2,32,1024]{2,1,0:T(8,128)(2,1)S(1)}, bf16[2,32,1024]{2,1,0:T(8,128)(2,1)S(1)}, u32[]{:S(2)}, u32[]{:S(2)}) collective-permute-start(bf16[2,32,1024]{2,1,0:T(8,128)(2,1)S(1)} %get-tuple-element.40), channel_id=1, source_target_pairs={{0,8},{4,12},{8,0},{12,4},{1,9},{5,13},{9,1},{13,5},{2,10},{6,14},... | collective-permute-start | bytes 393224 | tf_op jit(solution)/shard_map/ppermute | solution.py:169
  22.8 10.1 %collective-permute-start.4 = (bf16[2,32,1024]{2,1,0:T(8,128)(2,1)S(1)}, bf16[2,32,1024]{2,1,0:T(8,128)(2,1)S(1)}, u32[]{:S(2)}, u32[]{:S(2)}) collective-permute-start(bf16[2,32,1024]{2,1,0:T(8,128)(2,1)S(1)} %get-tuple-element.36), channel_id=1, source_target_pairs={{0,8},{4,12},{8,0},{12,4},{1,9},{5,13},{9,1},{13,5},{2,10},{6,14},... | collective-permute-start | bytes 393224 | tf_op jit(solution)/shard_map/ppermute | solution.py:169
  25.5 7.6 %collective-permute-start.14 = (bf16[32,1024]{1,0:T(8,128)(2,1)S(1)}, bf16[32,1024]{1,0:T(8,128)(2,1)S(1)}, u32[]{:S(2)}, u32[]{:S(2)}) collective-permute-start(bf16[32,1024]{1,0:T(8,128)(2,1)S(1)} %shard_map.76.mine_ref), channel_id=1, source_target_pairs={{0,4},{4,0},{8,12},{12,8},{1,5},{5,1},{9,13},{13,9},{2,6},{6,2},{1... | collective-permute-start | bytes 196616 | tf_op jit(solution)/shard_map/ppermute | solution.py:169
  28.3 5.5 %collective-permute-start.11 = (bf16[32,1024]{1,0:T(8,128)(2,1)S(1)}, bf16[32,1024]{1,0:T(8,128)(2,1)S(1)}, u32[]{:S(2)}, u32[]{:S(2)}) collective-permute-start(bf16[32,1024]{1,0:T(8,128)(2,1)S(1)} %shard_map.74.mine_ref), channel_id=1, source_target_pairs={{0,4},{4,0},{8,12},{12,8},{1,5},{5,1},{9,13},{13,9},{2,6},{6,2},{1... | collective-permute-start | bytes 196616 | tf_op jit(solution)/shard_map/ppermute | solution.py:169
  31.1 3.4 %collective-permute-start.8 = (bf16[32,1024]{1,0:T(8,128)(2,1)S(1)}, bf16[32,1024]{1,0:T(8,128)(2,1)S(1)}, u32[]{:S(2)}, u32[]{:S(2)}) collective-permute-start(bf16[32,1024]{1,0:T(8,128)(2,1)S(1)} %shard_map.71.mine_ref), channel_id=1, source_target_pairs={{0,4},{4,0},{8,12},{12,8},{1,5},{5,1},{9,13},{13,9},{2,6},{6,2},{1... | collective-permute-start | bytes 196616 | tf_op jit(solution)/shard_map/ppermute | solution.py:169
  33.0 2.1 %collective-permute-start.5 = (bf16[32,1024]{1,0:T(8,128)(2,1)S(1)}, bf16[32,1024]{1,0:T(8,128)(2,1)S(1)}, u32[]{:S(2)}, u32[]{:S(2)}) collective-permute-start(bf16[32,1024]{1,0:T(8,128)(2,1)S(1)} %shard_map.68.mine_ref), channel_id=1, source_target_pairs={{0,4},{4,0},{8,12},{12,8},{1,5},{5,1},{9,13},{13,9},{2,6},{6,2},{1... | collective-permute-start | bytes 196616 | tf_op jit(solution)/shard_map/ppermute | solution.py:169
  35.9 4.5 %collective-permute-start.15 = (bf16[16,1536]{1,0:T(8,128)(2,1)S(1)}, bf16[16,1536]{1,0:T(8,128)(2,1)S(1)}, u32[]{:S(2)}, u32[]{:S(2)}) collective-permute-start(bf16[16,1536]{1,0:T(8,128)(2,1)S(1)} %get-tuple-element.50), channel_id=1, source_target_pairs={{0,1},{1,0},{2,3},{3,2},{4,5},{5,4},{6,7},{7,6},{8,9},{9,8},{10,11... | collective-permute-start | bytes 147464 | tf_op jit(solution)/shard_map/ppermute | solution.py:169
  35.9 7.7 %collective-permute-start.16 = (bf16[16,1536]{1,0:T(8,128)(2,1)S(1)}, bf16[16,1536]{1,0:T(8,128)(2,1)S(1)}, u32[]{:S(2)}, u32[]{:S(2)}) collective-permute-start(bf16[16,1536]{1,0:T(8,128)(2,1)S(1)} %get-tuple-element.51), channel_id=1, source_target_pairs={{0,2},{1,3},{2,0},{3,1},{4,6},{5,7},{6,4},{7,5},{8,10},{9,11},{10,... | collective-permute-start | bytes 147464 | tf_op jit(solution)/shard_map/ppermute | solution.py:169
  37.2 6.4 %collective-permute-start.17 = (bf16[16,1536]{1,0:T(8,128)(2,1)S(1)}, bf16[16,1536]{1,0:T(8,128)(2,1)S(1)}, u32[]{:S(2)}, u32[]{:S(2)}) collective-permute-start(bf16[16,1536]{1,0:T(8,128)(2,1)S(1)} %get-tuple-element.52), channel_id=1, source_target_pairs={{0,3},{1,2},{2,1},{3,0},{4,7},{5,6},{6,5},{7,4},{8,11},{9,10},{10,... | collective-permute-start | bytes 147464 | tf_op jit(solution)/shard_map/ppermute | solution.py:169

commit v2 on v1

--- a/solution.py
+++ b/solution.py
@@ -82,15 +82,15 @@
     ).astype(BF16)
 
 
-def bit_order(spot):
-    return (spot % 2) * 2 + spot // 2
+def bit_order(spot, count):
+    return (spot % 2) * (count // 2) + spot // 2
 
 
 def gather_body(*refs):
     out_ref = refs[-1]
     place = (lax.axis_index("dp") % 2) ^ lax.axis_index("tp")
     for q, block in enumerate(refs[:-1]):
-        spot = bit_order(place ^ q)
+        spot = bit_order(place ^ q, len(refs) - 1)
         out_ref[pl.ds(pl.multiple_of(spot * MOST, MOST), MOST), :] = block[...]
 
 
@@ -138,7 +138,7 @@
     down_body(low, high, mine_ref, beside_ref, weight_ref, total_ref, scratch)
     place = (lax.axis_index("dp") % 2) ^ lax.axis_index("tp")
     for q in range(n_tp):
-        block = scratch[pl.ds(pl.multiple_of(bit_order(place ^ q) * MOST, MOST), MOST), :]
+        block = scratch[pl.ds(pl.multiple_of(bit_order(place ^ q, n_tp) * MOST, MOST), MOST), :]
         if q == 0:
             own_ref[...] = block
         else:
@@ -304,7 +304,7 @@
     def specialised(*args):
         return direct(n_dp, n_tp, *args)
 
-    fits = n_dp == n_tp == 4
+    fits = n_dp == 4 and n_tp in (2, 4, 8)
     return jax.shard_map(
         specialised if fits else general,
         mesh=mesh,

time: 44.6 us -> 44.6 us (level)
  no operation moved by 1% of the time
where the time goes in v2:
time: 44.6 us; the launch traced here: 44.4 us
  waiting for transfers between devices  18.3 us (41%)
  starting transfers between devices  16 us (36%)
  Pallas kernels  9.9 us (22%)
    ppermute x18, waiting for transfers between devices, swap(): return lax.ppermute(value, axis, [(i, i ^ mask) for i in range(size)])  18.3 us
    ppermute x18, starting transfers between devices, swap(): return lax.ppermute(value, axis, [(i, i ^ mask) for i in range(size)])  16 us
    pallas_call x18, Pallas kernels, call(): pl.pallas_call(body, out_shape=outs, in_specs=[spec] * len(args), out_spe...  9.9 us
  transfers between devices with their start and end apart: 18, of which 7 were waited for; matrix products, arithmetic and copies ran while one was open for 0% of the time, Pallas kernels for 13%

profile of v2, /device:TPU:0, one launch (start us, length us, event | category | flops | bytes accessed | tf_op | source)
XLA Modules:
  0.0 44.4 jit_solution(3612996350948466787)
XLA Ops:
  0.0 1.2 %shard_map.64 = (bf16[16,1536]{1,0:T(8,128)(2,1)S(1)}, bf16[32,96]{1,0:T(8,128)(2,1)S(1)}, f32[32,1]{1,0:T(8,128)S(1)}) custom-call(s32[2,32]{1,0:T(2,128)} %bitcast.4, f32[2,32]{1,0:T(2,128)} %bitcast.5, bf16[32,1536]{1,0:T(8,128)(2,1)} %tokens_hbm.1), custom_call_target="tpu_custom_call" | custom-call | flops 40265318400000 | bytes 629145600000 | tf_op jit(solution)/shard_map/pallas_call | solution.py:23
  1.3 3.1 %collective-permute-start = (bf16[16,1536]{1,0:T(8,128)(2,1)S(1)}, bf16[16,1536]{1,0:T(8,128)(2,1)S(1)}, u32[]{:S(2)}, u32[]{:S(2)}) collective-permute-start(bf16[16,1536]{1,0:T(8,128)(2,1)S(1)} %get-tuple-element.31.refs_0_), channel_id=1, source_target_pairs={{0,1},{1,0},{2,3},{3,2},{4,5},{5,4},{6,7},{7,6},{8,9},{9,8},{10,11... | collective-permute-start | bytes 147464 | tf_op jit(solution)/shard_map/ppermute | solution.py:169
  4.4 2.6 %collective-permute-start.1 = (bf16[16,1536]{1,0:T(8,128)(2,1)S(1)}, bf16[16,1536]{1,0:T(8,128)(2,1)S(1)}, u32[]{:S(2)}, u32[]{:S(2)}) collective-permute-start(bf16[16,1536]{1,0:T(8,128)(2,1)S(1)} %get-tuple-element.31.refs_0_), channel_id=1, source_target_pairs={{0,2},{1,3},{2,0},{3,1},{4,6},{5,7},{6,4},{7,5},{8,10},{9,11},{10,... | collective-permute-start | bytes 147464 | tf_op jit(solution)/shard_map/ppermute | solution.py:169
  7.0 0.0 collective-permute-start.2
  7.0 0.0 collective-permute-done.refs_1_
  7.0 3.3 %collective-permute-done.1.refs_2_ = bf16[16,1536]{1,0:T(8,128)(2,1)S(1)} collective-permute-done((bf16[16,1536]{1,0:T(8,128)(2,1)S(1)}, bf16[16,1536]{1,0:T(8,128)(2,1)S(1)}, u32[]{:S(2)}, u32[]{:S(2)}) %collective-permute-start.1) | collective-permute-done | bytes 49184 | tf_op jit(solution)/shard_map/ppermute | solution.py:169
  10.3 2.6 %collective-permute-done.2.refs_3_ = bf16[16,1536]{1,0:T(8,128)(2,1)S(1)} collective-permute-done((bf16[16,1536]{1,0:T(8,128)(2,1)S(1)}, bf16[16,1536]{1,0:T(8,128)(2,1)S(1)}, u32[]{:S(2)}, u32[]{:S(2)}) %collective-permute-start.2) | collective-permute-done | bytes 49184 | tf_op jit(solution)/shard_map/ppermute | solution.py:169
  12.9 1.2 %shard_map.65 = (bf16[2,32,1024]{2,1,0:T(8,128)(2,1)S(1)}, bf16[2,32,1024]{2,1,0:T(8,128)(2,1)S(1)}, bf16[64,1536]{1,0:T(8,128)(2,1)S(1)}) custom-call(bf16[16,1536]{1,0:T(8,128)(2,1)S(1)} %get-tuple-element.31.refs_0_, bf16[16,1536]{1,0:T(8,128)(2,1)S(1)} %collective-permute-done.refs_1_, bf16[16,1536]{1,0:T(8,128)(2,1)S(1)} %collective-permute-done.1.refs_2_, ...), custom_call_target="tpu_custom_call" | custom-call | flops 402653184 | bytes 6291456 | tf_op jit(solution)/shard_map/pallas_call | solution.py:23
  14.1 0.1 collective-permute-start.12
  14.1 1.2 %shard_map.72 = (bf16[2,32,1024]{2,1,0:T(8,128)(2,1)S(1)}, bf16[2,32,1024]{2,1,0:T(8,128)(2,1)S(1)}) custom-call(bf16[64,1536]{1,0:T(8,128)(2,1)S(1)} %get-tuple-element.32.rows_ref, bf16[1536,4096]{1,0:T(8,128)(2,1)S(1)} %copy-done, bf16[1536,4096]{1,0:T(8,128)(2,1)S(1)} %copy-done.1), custom_call_target="tpu_custom_call" | custom-call | flops 402653184 | bytes 6291456 | tf_op jit(solution)/shard_map/pallas_call | solution.py:23
  15.4 0.0 slice-start
  15.4 0.0 slice-start.1
  15.4 1.2 %shard_map.69 = (bf16[2,32,1024]{2,1,0:T(8,128)(2,1)S(1)}, bf16[2,32,1024]{2,1,0:T(8,128)(2,1)S(1)}) custom-call(bf16[64,1536]{1,0:T(8,128)(2,1)S(1)} %get-tuple-element.32.rows_ref, bf16[1536,4096]{1,0:T(8,128)(2,1)S(1)} %copy-done, bf16[1536,4096]{1,0:T(8,128)(2,1)S(1)} %copy-done.1), custom_call_target="tpu_custom_call" | custom-call | flops 402653184 | bytes 6291456 | tf_op jit(solution)/shard_map/pallas_call | solution.py:23
  16.6 0.0 slice-start.2
  16.6 0.6 %collective-permute-start.9 = (bf16[2,32,1024]{2,1,0:T(8,128)(2,1)S(1)}, bf16[2,32,1024]{2,1,0:T(8,128)(2,1)S(1)}, u32[]{:S(2)}, u32[]{:S(2)}) collective-permute-start(bf16[2,32,1024]{2,1,0:T(8,128)(2,1)S(1)} %get-tuple-element.42), channel_id=1, source_target_pairs={{0,4},{4,0},{8,12},{12,8},{1,5},{5,1},{9,13},{13,9},{2,6},{6,2},{1... | collective-permute-start | bytes 393224 | tf_op jit(solution)/shard_map/ppermute | solution.py:169
  17.2 0.1 collective-permute-start.6
  17.2 1.2 %shard_map.66 = (bf16[2,32,1024]{2,1,0:T(8,128)(2,1)S(1)}, bf16[2,32,1024]{2,1,0:T(8,128)(2,1)S(1)}) custom-call(bf16[64,1536]{1,0:T(8,128)(2,1)S(1)} %get-tuple-element.32.rows_ref, bf16[1536,4096]{1,0:T(8,128)(2,1)S(1)} %copy-done, bf16[1536,4096]{1,0:T(8,128)(2,1)S(1)} %copy-done.1), custom_call_target="tpu_custom_call" | custom-call | flops 402653184 | bytes 6291456 | tf_op jit(solution)/shard_map/pallas_call | solution.py:23
  18.4 0.5 %collective-permute-start.3 = (bf16[2,32,1024]{2,1,0:T(8,128)(2,1)S(1)}, bf16[2,32,1024]{2,1,0:T(8,128)(2,1)S(1)}, u32[]{:S(2)}, u32[]{:S(2)}) collective-permute-start(bf16[2,32,1024]{2,1,0:T(8,128)(2,1)S(1)} %get-tuple-element.34), channel_id=1, source_target_pairs={{0,4},{4,0},{8,12},{12,8},{1,5},{5,1},{9,13},{13,9},{2,6},{6,2},{1... | collective-permute-start | bytes 393224 | tf_op jit(solution)/shard_map/ppermute | solution.py:169
  18.9 0.0 collective-permute-done.12.got_ref
  19.0 1.6 %collective-permute-start.13 = (bf16[2,32,1024]{2,1,0:T(8,128)(2,1)S(1)}, bf16[2,32,1024]{2,1,0:T(8,128)(2,1)S(1)}, u32[]{:S(2)}, u32[]{:S(2)}) collective-permute-start(bf16[2,32,1024]{2,1,0:T(8,128)(2,1)S(1)} %get-tuple-element.48), channel_id=1, source_target_pairs={{0,8},{4,12},{8,0},{12,4},{1,9},{5,13},{9,1},{13,5},{2,10},{6,14},... | collective-permute-start | bytes 393224 | tf_op jit(solution)/shard_map/ppermute | solution.py:169
  20.6 0.6 %collective-permute-start.10 = (bf16[2,32,1024]{2,1,0:T(8,128)(2,1)S(1)}, bf16[2,32,1024]{2,1,0:T(8,128)(2,1)S(1)}, u32[]{:S(2)}, u32[]{:S(2)}) collective-permute-start(bf16[2,32,1024]{2,1,0:T(8,128)(2,1)S(1)} %get-tuple-element.44), channel_id=1, source_target_pairs={{0,8},{4,12},{8,0},{12,4},{1,9},{5,13},{9,1},{13,5},{2,10},{6,14},... | collective-permute-start | bytes 393224 | tf_op jit(solution)/shard_map/ppermute | solution.py:169
  21.2 0.0 collective-permute-done.6.got_ref
  21.2 1.6 %collective-permute-start.7 = (bf16[2,32,1024]{2,1,0:T(8,128)(2,1)S(1)}, bf16[2,32,1024]{2,1,0:T(8,128)(2,1)S(1)}, u32[]{:S(2)}, u32[]{:S(2)}) collective-permute-start(bf16[2,32,1024]{2,1,0:T(8,128)(2,1)S(1)} %get-tuple-element.40), channel_id=1, source_target_pairs={{0,8},{4,12},{8,0},{12,4},{1,9},{5,13},{9,1},{13,5},{2,10},{6,14},... | collective-permute-start | bytes 393224 | tf_op jit(solution)/shard_map/ppermute | solution.py:169
  22.8 0.6 %collective-permute-start.4 = (bf16[2,32,1024]{2,1,0:T(8,128)(2,1)S(1)}, bf16[2,32,1024]{2,1,0:T(8,128)(2,1)S(1)}, u32[]{:S(2)}, u32[]{:S(2)}) collective-permute-start(bf16[2,32,1024]{2,1,0:T(8,128)(2,1)S(1)} %get-tuple-element.36), channel_id=1, source_target_pairs={{0,8},{4,12},{8,0},{12,4},{1,9},{5,13},{9,1},{13,5},{2,10},{6,14},... | collective-permute-start | bytes 393224 | tf_op jit(solution)/shard_map/ppermute | solution.py:169
  23.4 2.0 %collective-permute-done.13.got_ref = bf16[2,32,1024]{2,1,0:T(8,128)(2,1)S(1)} collective-permute-done((bf16[2,32,1024]{2,1,0:T(8,128)(2,1)S(1)}, bf16[2,32,1024]{2,1,0:T(8,128)(2,1)S(1)}, u32[]{:S(2)}, u32[]{:S(2)}) %collective-permute-start.13) | collective-permute-done | bytes 131104 | tf_op jit(solution)/shard_map/ppermute | solution.py:169
  25.4 0.1 shard_map.76.mine_ref
  25.5 0.1 collective-permute-start.14
  25.6 2.7 %collective-permute-done.10.got_ref = bf16[2,32,1024]{2,1,0:T(8,128)(2,1)S(1)} collective-permute-done((bf16[2,32,1024]{2,1,0:T(8,128)(2,1)S(1)}, bf16[2,32,1024]{2,1,0:T(8,128)(2,1)S(1)}, u32[]{:S(2)}, u32[]{:S(2)}) %collective-permute-start.10) | collective-permute-done | bytes 131104 | tf_op jit(solution)/shard_map/ppermute | solution.py:169
  28.2 0.1 shard_map.74.mine_ref
  28.3 0.1 collective-permute-start.11
  28.4 2.7 %collective-permute-done.7.got_ref = bf16[2,32,1024]{2,1,0:T(8,128)(2,1)S(1)} collective-permute-done((bf16[2,32,1024]{2,1,0:T(8,128)(2,1)S(1)}, bf16[2,32,1024]{2,1,0:T(8,128)(2,1)S(1)}, u32[]{:S(2)}, u32[]{:S(2)}) %collective-permute-start.7) | collective-permute-done | bytes 131104 | tf_op jit(solution)/shard_map/ppermute | solution.py:169
  31.0 0.1 shard_map.71.mine_ref
  31.1 0.1 collective-permute-start.8
  31.2 1.8 %collective-permute-done.4.got_ref = bf16[2,32,1024]{2,1,0:T(8,128)(2,1)S(1)} collective-permute-done((bf16[2,32,1024]{2,1,0:T(8,128)(2,1)S(1)}, bf16[2,32,1024]{2,1,0:T(8,128)(2,1)S(1)}, u32[]{:S(2)}, u32[]{:S(2)}) %collective-permute-start.4) | collective-permute-done | bytes 131104 | tf_op jit(solution)/shard_map/ppermute | solution.py:169
  33.0 0.1 shard_map.68.mine_ref
  33.0 0.1 collective-permute-start.5
  33.1 0.0 collective-permute-done.14.beside_ref
  33.1 0.6 %shard_map.77.refs_0_ = f32[64,1536]{1,0:T(8,128)S(1)} custom-call(bf16[32,1024]{1,0:T(8,128)(2,1)S(1)} %shard_map.76.mine_ref, bf16[32,1024]{1,0:T(8,128)(2,1)S(1)} %collective-permute-done.14.beside_ref, bf16[4096,1536]{1,0:T(8,128)(2,1)S(1)} %bitcast.3), custom_call_target="tpu_custom_call" | custom-call | flops 201326592 | bytes 3145728 | tf_op jit(solution)/shard_map/pallas_call | solution.py:23
  33.8 0.0 collective-permute-done.11.beside_ref
  33.8 0.7 %shard_map.78.refs_0_ = f32[64,1536]{1,0:T(8,128)S(1)} custom-call(bf16[32,1024]{1,0:T(8,128)(2,1)S(1)} %shard_map.74.mine_ref, bf16[32,1024]{1,0:T(8,128)(2,1)S(1)} %collective-permute-done.11.beside_ref, bf16[4096,1536]{1,0:T(8,128)(2,1)S(1)} %bitcast.3, f32[64,1536]{1,0:T(8,128)S(1)} %shard_map.77.refs_0_), custom_call_target="tpu_custom_call" | custom-call | flops 201326592 | bytes 3145728 | tf_op jit(solution)/shard_map/pallas_call | solution.py:23
  34.5 0.7 %shard_map.79.total_ref = f32[64,1536]{1,0:T(8,128)S(1)} custom-call(bf16[32,1024]{1,0:T(8,128)(2,1)S(1)} %shard_map.71.mine_ref, bf16[32,1024]{1,0:T(8,128)(2,1)S(1)} %collective-permute-done.8.beside_ref, bf16[4096,1536]{1,0:T(8,128)(2,1)S(1)} %bitcast.3, f32[64,1536]{1,0:T(8,128)S(1)} %shard_map.78.refs_0_), custom_call_target="tpu_custom_call" | custom-call | flops 201326592 | bytes 3145728 | tf_op jit(solution)/shard_map/pallas_call | solution.py:23
  35.2 0.0 collective-permute-done.5.beside_ref
  35.2 0.7 %shard_map.80 = (f32[16,1536]{1,0:T(8,128)S(1)}, bf16[16,1536]{1,0:T(8,128)(2,1)S(1)}, bf16[16,1536]{1,0:T(8,128)(2,1)S(1)}, bf16[16,1536]{1,0:T(8,128)(2,1)S(1)}) custom-call(bf16[32,1024]{1,0:T(8,128)(2,1)S(1)} %shard_map.68.mine_ref, bf16[32,1024]{1,0:T(8,128)(2,1)S(1)} %collective-permute-done.5.beside_ref, bf16[4096,1536]{1,0:T(8,128)(2,1)S(1)} %bitcast.3, ...), custom_call_target="tpu_custom_call" | custom-call | flops 201326592 | bytes 3145728 | tf_op jit(solution)/shard_map/pallas_call | solution.py:23
  35.9 0.1 collective-permute-start.15
  35.9 1.3 %collective-permute-start.16 = (bf16[16,1536]{1,0:T(8,128)(2,1)S(1)}, bf16[16,1536]{1,0:T(8,128)(2,1)S(1)}, u32[]{:S(2)}, u32[]{:S(2)}) collective-permute-start(bf16[16,1536]{1,0:T(8,128)(2,1)S(1)} %get-tuple-element.51), channel_id=1, source_target_pairs={{0,2},{1,3},{2,0},{3,1},{4,6},{5,7},{6,4},{7,5},{8,10},{9,11},{10,... | collective-permute-start | bytes 147464 | tf_op jit(solution)/shard_map/ppermute | solution.py:169
  37.2 3.1 %collective-permute-start.17 = (bf16[16,1536]{1,0:T(8,128)(2,1)S(1)}, bf16[16,1536]{1,0:T(8,128)(2,1)S(1)}, u32[]{:S(2)}, u32[]{:S(2)}) collective-permute-start(bf16[16,1536]{1,0:T(8,128)(2,1)S(1)} %get-tuple-element.52), channel_id=1, source_target_pairs={{0,3},{1,2},{2,1},{3,0},{4,7},{5,6},{6,5},{7,4},{8,11},{9,10},{10,... | collective-permute-start | bytes 147464 | tf_op jit(solution)/shard_map/ppermute | solution.py:169
  40.3 3.3 %collective-permute-done.16.refs_1_ = bf16[16,1536]{1,0:T(8,128)(2,1)S(1)} collective-permute-done((bf16[16,1536]{1,0:T(8,128)(2,1)S(1)}, bf16[16,1536]{1,0:T(8,128)(2,1)S(1)}, u32[]{:S(2)}, u32[]{:S(2)}) %collective-permute-start.16) | collective-permute-done | bytes 49184 | tf_op jit(solution)/shard_map/ppermute | solution.py:169
  43.6 0.8 %shard_map.81 = bf16[32,1536]{1,0:T(8,128)(2,1)} custom-call(bf16[32,96]{1,0:T(8,128)(2,1)S(1)} %get-tuple-element.29.slots_ref, f32[32,1]{1,0:T(8,128)S(1)} %get-tuple-element.30.combine_ref, f32[16,1536]{1,0:T(8,128)S(1)} %get-tuple-element.49.own_ref, bf16[16,1536]{1,0:T(8,128)(2,1)S(1)} %collective-permute-done.15.refs_0_, ...), custom_call_target="tpu_custom_call" | custom-call | flops 98304 | bytes 196608 | tf_op jit(solution)/shard_map/pallas_call | solution.py:23
  (17 shorter events, 0.2 us)
Async XLA Ops:
  0.0 12.9 %copy-start = (bf16[1536,4096]{1,0:T(8,128)(2,1)S(1)}, bf16[1536,4096]{1,0:T(8,128)(2,1)}, u32[]{:S(2)}) copy-start(bf16[1536,4096]{1,0:T(8,128)(2,1)} %gate_ref.5) | copy-start | bytes 37748740
  0.0 12.9 %copy-start.1 = (bf16[1536,4096]{1,0:T(8,128)(2,1)S(1)}, bf16[1536,4096]{1,0:T(8,128)(2,1)}, u32[]{:S(2)}) copy-start(bf16[1536,4096]{1,0:T(8,128)(2,1)} %up_ref.5) | copy-start | bytes 37748740
  1.3 5.7 %collective-permute-start = (bf16[16,1536]{1,0:T(8,128)(2,1)S(1)}, bf16[16,1536]{1,0:T(8,128)(2,1)S(1)}, u32[]{:S(2)}, u32[]{:S(2)}) collective-permute-start(bf16[16,1536]{1,0:T(8,128)(2,1)S(1)} %get-tuple-element.31.refs_0_), channel_id=1, source_target_pairs={{0,1},{1,0},{2,3},{3,2},{4,5},{5,4},{6,7},{7,6},{8,9},{9,8},{10,11... | collective-permute-start | bytes 147464 | tf_op jit(solution)/shard_map/ppermute | solution.py:169
  4.4 5.9 %collective-permute-start.1 = (bf16[16,1536]{1,0:T(8,128)(2,1)S(1)}, bf16[16,1536]{1,0:T(8,128)(2,1)S(1)}, u32[]{:S(2)}, u32[]{:S(2)}) collective-permute-start(bf16[16,1536]{1,0:T(8,128)(2,1)S(1)} %get-tuple-element.31.refs_0_), channel_id=1, source_target_pairs={{0,2},{1,3},{2,0},{3,1},{4,6},{5,7},{6,4},{7,5},{8,10},{9,11},{10,... | collective-permute-start | bytes 147464 | tf_op jit(solution)/shard_map/ppermute | solution.py:169
  7.0 5.9 %collective-permute-start.2 = (bf16[16,1536]{1,0:T(8,128)(2,1)S(1)}, bf16[16,1536]{1,0:T(8,128)(2,1)S(1)}, u32[]{:S(2)}, u32[]{:S(2)}) collective-permute-start(bf16[16,1536]{1,0:T(8,128)(2,1)S(1)} %get-tuple-element.31.refs_0_), channel_id=1, source_target_pairs={{0,3},{1,2},{2,1},{3,0},{4,7},{5,6},{6,5},{7,4},{8,11},{9,10},{10,... | collective-permute-start | bytes 147464 | tf_op jit(solution)/shard_map/ppermute | solution.py:169
  14.1 4.9 %collective-permute-start.12 = (bf16[2,32,1024]{2,1,0:T(8,128)(2,1)S(1)}, bf16[2,32,1024]{2,1,0:T(8,128)(2,1)S(1)}, u32[]{:S(2)}, u32[]{:S(2)}) collective-permute-start(bf16[2,32,1024]{2,1,0:T(8,128)(2,1)S(1)} %get-tuple-element.46), channel_id=1, source_target_pairs={{0,4},{4,0},{8,12},{12,8},{1,5},{5,1},{9,13},{13,9},{2,6},{6,2},{1... | collective-permute-start | bytes 393224 | tf_op jit(solution)/shard_map/ppermute | solution.py:169
  15.4 17.8 %slice-start = ((s8[12582912]{0:T(1024)(128)(4,1)}), s8[4194304]{0:T(1024)(128)(4,1)S(1)}, s32[]{:S(2)}) async-start(s8[12582912]{0:T(1024)(128)(4,1)} %bitcast.2), calls=%async_computation | async-start | bytes 8388608
  15.4 17.8 %slice-start.1 = ((s8[12582912]{0:T(1024)(128)(4,1)}), s8[4194304]{0:T(1024)(128)(4,1)S(1)}, s32[]{:S(2)}) async-start(s8[12582912]{0:T(1024)(128)(4,1)} %bitcast.2), calls=%async_computation.1 | async-start | bytes 8388608
  16.6 16.5 %slice-start.2 = ((s8[12582912]{0:T(1024)(128)(4,1)}), s8[4194304]{0:T(1024)(128)(4,1)S(1)}, s32[]{:S(2)}) async-start(s8[12582912]{0:T(1024)(128)(4,1)} %bitcast.2), calls=%async_computation.2 | async-start | bytes 8388608
  16.6 3.9 %collective-permute-start.9 = (bf16[2,32,1024]{2,1,0:T(8,128)(2,1)S(1)}, bf16[2,32,1024]{2,1,0:T(8,128)(2,1)S(1)}, u32[]{:S(2)}, u32[]{:S(2)}) collective-permute-start(bf16[2,32,1024]{2,1,0:T(8,128)(2,1)S(1)} %get-tuple-element.42), channel_id=1, source_target_pairs={{0,4},{4,0},{8,12},{12,8},{1,5},{5,1},{9,13},{13,9},{2,6},{6,2},{1... | collective-permute-start | bytes 393224 | tf_op jit(solution)/shard_map/ppermute | solution.py:169
  17.2 4.0 %collective-permute-start.6 = (bf16[2,32,1024]{2,1,0:T(8,128)(2,1)S(1)}, bf16[2,32,1024]{2,1,0:T(8,128)(2,1)S(1)}, u32[]{:S(2)}, u32[]{:S(2)}) collective-permute-start(bf16[2,32,1024]{2,1,0:T(8,128)(2,1)S(1)} %get-tuple-element.38), channel_id=1, source_target_pairs={{0,4},{4,0},{8,12},{12,8},{1,5},{5,1},{9,13},{13,9},{2,6},{6,2},{1... | collective-permute-start | bytes 393224 | tf_op jit(solution)/shard_map/ppermute | solution.py:169
  18.4 4.4 %collective-permute-start.3 = (bf16[2,32,1024]{2,1,0:T(8,128)(2,1)S(1)}, bf16[2,32,1024]{2,1,0:T(8,128)(2,1)S(1)}, u32[]{:S(2)}, u32[]{:S(2)}) collective-permute-start(bf16[2,32,1024]{2,1,0:T(8,128)(2,1)S(1)} %get-tuple-element.34), channel_id=1, source_target_pairs={{0,4},{4,0},{8,12},{12,8},{1,5},{5,1},{9,13},{13,9},{2,6},{6,2},{1... | collective-permute-start | bytes 393224 | tf_op jit(solution)/shard_map/ppermute | solution.py:169
  19.0 6.4 %collective-permute-start.13 = (bf16[2,32,1024]{2,1,0:T(8,128)(2,1)S(1)}, bf16[2,32,1024]{2,1,0:T(8,128)(2,1)S(1)}, u32[]{:S(2)}, u32[]{:S(2)}) collective-permute-start(bf16[2,32,1024]{2,1,0:T(8,128)(2,1)S(1)} %get-tuple-element.48), channel_id=1, source_target_pairs={{0,8},{4,12},{8,0},{12,4},{1,9},{5,13},{9,1},{13,5},{2,10},{6,14},... | collective-permute-start | bytes 393224 | tf_op jit(solution)/shard_map/ppermute | solution.py:169
  20.6 7.6 %collective-permute-start.10 = (bf16[2,32,1024]{2,1,0:T(8,128)(2,1)S(1)}, bf16[2,32,1024]{2,1,0:T(8,128)(2,1)S(1)}, u32[]{:S(2)}, u32[]{:S(2)}) collective-permute-start(bf16[2,32,1024]{2,1,0:T(8,128)(2,1)S(1)} %get-tuple-element.44), channel_id=1, source_target_pairs={{0,8},{4,12},{8,0},{12,4},{1,9},{5,13},{9,1},{13,5},{2,10},{6,14},... | collective-permute-start | bytes 393224 | tf_op jit(solution)/shard_map/ppermute | solution.py:169
  21.2 9.8 %collective-permute-start.7 = (bf16[2,32,1024]{2,1,0:T(8,128)(2,1)S(1)}, bf16[2,32,1024]{2,1,0:T(8,128)(2,1)S(1)}, u32[]{:S(2)}, u32[]{:S(2)}) collective-permute-start(bf16[2,32,1024]{2,1,0:T(8,128)(2,1)S(1)} %get-tuple-element.40), channel_id=1, source_target_pairs={{0,8},{4,12},{8,0},{12,4},{1,9},{5,13},{9,1},{13,5},{2,10},{6,14},... | collective-permute-start | bytes 393224 | tf_op jit(solution)/shard_map/ppermute | solution.py:169
  22.8 10.1 %collective-permute-start.4 = (bf16[2,32,1024]{2,1,0:T(8,128)(2,1)S(1)}, bf16[2,32,1024]{2,1,0:T(8,128)(2,1)S(1)}, u32[]{:S(2)}, u32[]{:S(2)}) collective-permute-start(bf16[2,32,1024]{2,1,0:T(8,128)(2,1)S(1)} %get-tuple-element.36), channel_id=1, source_target_pairs={{0,8},{4,12},{8,0},{12,4},{1,9},{5,13},{9,1},{13,5},{2,10},{6,14},... | collective-permute-start | bytes 393224 | tf_op jit(solution)/shard_map/ppermute | solution.py:169
  25.5 7.6 %collective-permute-start.14 = (bf16[32,1024]{1,0:T(8,128)(2,1)S(1)}, bf16[32,1024]{1,0:T(8,128)(2,1)S(1)}, u32[]{:S(2)}, u32[]{:S(2)}) collective-permute-start(bf16[32,1024]{1,0:T(8,128)(2,1)S(1)} %shard_map.76.mine_ref), channel_id=1, source_target_pairs={{0,4},{4,0},{8,12},{12,8},{1,5},{5,1},{9,13},{13,9},{2,6},{6,2},{1... | collective-permute-start | bytes 196616 | tf_op jit(solution)/shard_map/ppermute | solution.py:169
  28.3 5.5 %collective-permute-start.11 = (bf16[32,1024]{1,0:T(8,128)(2,1)S(1)}, bf16[32,1024]{1,0:T(8,128)(2,1)S(1)}, u32[]{:S(2)}, u32[]{:S(2)}) collective-permute-start(bf16[32,1024]{1,0:T(8,128)(2,1)S(1)} %shard_map.74.mine_ref), channel_id=1, source_target_pairs={{0,4},{4,0},{8,12},{12,8},{1,5},{5,1},{9,13},{13,9},{2,6},{6,2},{1... | collective-permute-start | bytes 196616 | tf_op jit(solution)/shard_map/ppermute | solution.py:169
  31.1 3.4 %collective-permute-start.8 = (bf16[32,1024]{1,0:T(8,128)(2,1)S(1)}, bf16[32,1024]{1,0:T(8,128)(2,1)S(1)}, u32[]{:S(2)}, u32[]{:S(2)}) collective-permute-start(bf16[32,1024]{1,0:T(8,128)(2,1)S(1)} %shard_map.71.mine_ref), channel_id=1, source_target_pairs={{0,4},{4,0},{8,12},{12,8},{1,5},{5,1},{9,13},{13,9},{2,6},{6,2},{1... | collective-permute-start | bytes 196616 | tf_op jit(solution)/shard_map/ppermute | solution.py:169
  33.0 2.1 %collective-permute-start.5 = (bf16[32,1024]{1,0:T(8,128)(2,1)S(1)}, bf16[32,1024]{1,0:T(8,128)(2,1)S(1)}, u32[]{:S(2)}, u32[]{:S(2)}) collective-permute-start(bf16[32,1024]{1,0:T(8,128)(2,1)S(1)} %shard_map.68.mine_ref), channel_id=1, source_target_pairs={{0,4},{4,0},{8,12},{12,8},{1,5},{5,1},{9,13},{13,9},{2,6},{6,2},{1... | collective-permute-start | bytes 196616 | tf_op jit(solution)/shard_map/ppermute | solution.py:169
  35.9 4.5 %collective-permute-start.15 = (bf16[16,1536]{1,0:T(8,128)(2,1)S(1)}, bf16[16,1536]{1,0:T(8,128)(2,1)S(1)}, u32[]{:S(2)}, u32[]{:S(2)}) collective-permute-start(bf16[16,1536]{1,0:T(8,128)(2,1)S(1)} %get-tuple-element.50), channel_id=1, source_target_pairs={{0,1},{1,0},{2,3},{3,2},{4,5},{5,4},{6,7},{7,6},{8,9},{9,8},{10,11... | collective-permute-start | bytes 147464 | tf_op jit(solution)/shard_map/ppermute | solution.py:169
  35.9 7.7 %collective-permute-start.16 = (bf16[16,1536]{1,0:T(8,128)(2,1)S(1)}, bf16[16,1536]{1,0:T(8,128)(2,1)S(1)}, u32[]{:S(2)}, u32[]{:S(2)}) collective-permute-start(bf16[16,1536]{1,0:T(8,128)(2,1)S(1)} %get-tuple-element.51), channel_id=1, source_target_pairs={{0,2},{1,3},{2,0},{3,1},{4,6},{5,7},{6,4},{7,5},{8,10},{9,11},{10,... | collective-permute-start | bytes 147464 | tf_op jit(solution)/shard_map/ppermute | solution.py:169
  37.2 6.4 %collective-permute-start.17 = (bf16[16,1536]{1,0:T(8,128)(2,1)S(1)}, bf16[16,1536]{1,0:T(8,128)(2,1)S(1)}, u32[]{:S(2)}, u32[]{:S(2)}) collective-permute-start(bf16[16,1536]{1,0:T(8,128)(2,1)S(1)} %get-tuple-element.52), channel_id=1, source_target_pairs={{0,3},{1,2},{2,1},{3,0},{4,7},{5,6},{6,5},{7,4},{8,11},{9,10},{10,... | collective-permute-start | bytes 147464 | tf_op jit(solution)/shard_map/ppermute | solution.py:169

commit v3 on v2

--- a/solution.py
+++ b/solution.py
@@ -115,14 +115,12 @@
     gate_up(rows_ref[...], (gate_ref, up_ref), keep_ref, send_ref, low, high)
 
 
-def fold_body(keep_ref, got_ref, own_ref, send_ref):
-    total = keep_ref[...].astype(F32) + got_ref[...].astype(F32)
-    own_ref[...] = total
-    send_ref[...] = total.astype(BF16)
-
-
-def hidden_body(own_ref, got_ref, out_ref):
-    total = own_ref[...] + got_ref[...].astype(F32)
+def fold_body(keep_ref, got_ref, send_ref):
+    send_ref[...] = (keep_ref[...].astype(F32) + got_ref[...].astype(F32)).astype(BF16)
+
+
+def hidden_body(keep_ref, pair_ref, cross_ref, out_ref):
+    total = keep_ref[...].astype(F32) + pair_ref[...].astype(F32) + cross_ref[...].astype(F32)
     gate, up = total[0], total[1]
     out_ref[...] = (gate / (1.0 + jnp.exp(-gate)) * up).astype(BF16)
 
@@ -221,14 +219,14 @@
             )
         got = swap(send, "dp", n_dp, 1)
         folded.append(
-            call(fold_body, [shape(dims, F32), shape(dims, BF16)], total * width, 6 * total * width, keep, got)
+            (keep, got, call(fold_body, shape(dims, BF16), total * width, 6 * total * width, keep, got))
         )
     value = []
     for c, (low, high) in enumerate(spans):
-        own, send = folded[c]
+        keep, pair, send = folded[c]
         got = swap(send, "dp", n_dp, 2)
         mine = call(
-            hidden_body, shape(own.shape[1:], BF16), total * width, 3 * total * width, own, got
+            hidden_body, shape(send.shape[1:], BF16), total * width, 3 * total * width, keep, pair, got
         )
         beside = swap(mine, "dp", n_dp, 1)
         cost = 2 * total * (high - low) * out_width, 2 * (high - low) * out_width

time: 44.6 us -> 44.6 us (level)
  transfers between devices with their start and end apart: 18 -> 18, of which waited for: 7 -> 7; matrix products, arithmetic and copies ran while one was open for 0% -> 0% of each run, Pallas kernels for 13% -> 14%
where the time goes in v3:
time: 44.6 us; the launch traced here: 44.5 us
  waiting for transfers between devices  18.2 us (41%)
  starting transfers between devices  16 us (36%)
  Pallas kernels  9.98 us (22%)
    ppermute x18, waiting for transfers between devices, swap(): return lax.ppermute(value, axis, [(i, i ^ mask) for i in range(size)])  18.2 us
    ppermute x18, starting transfers between devices, swap(): return lax.ppermute(value, axis, [(i, i ^ mask) for i in range(size)])  16 us
    pallas_call x18, Pallas kernels, call(): pl.pallas_call(body, out_shape=outs, in_specs=[spec] * len(args), out_spe...  9.98 us
  transfers between devices with their start and end apart: 18, of which 7 were waited for; matrix products, arithmetic and copies ran while one was open for 0% of the time, Pallas kernels for 14%

profile of v3, /device:TPU:0, one launch (start us, length us, event | category | flops | bytes accessed | tf_op | source)
XLA Modules:
  0.0 44.5 jit_solution(14245509089757558708)
XLA Ops:
  0.0 1.2 %shard_map.64 = (bf16[16,1536]{1,0:T(8,128)(2,1)S(1)}, bf16[32,96]{1,0:T(8,128)(2,1)S(1)}, f32[32,1]{1,0:T(8,128)S(1)}) custom-call(s32[2,32]{1,0:T(2,128)} %bitcast.4, f32[2,32]{1,0:T(2,128)} %bitcast.5, bf16[32,1536]{1,0:T(8,128)(2,1)} %tokens_hbm.1), custom_call_target="tpu_custom_call" | custom-call | flops 40265318400000 | bytes 629145600000 | tf_op jit(solution)/shard_map/pallas_call | solution.py:23
  1.3 3.1 %collective-permute-start = (bf16[16,1536]{1,0:T(8,128)(2,1)S(1)}, bf16[16,1536]{1,0:T(8,128)(2,1)S(1)}, u32[]{:S(2)}, u32[]{:S(2)}) collective-permute-start(bf16[16,1536]{1,0:T(8,128)(2,1)S(1)} %get-tuple-element.23.refs_0_), channel_id=1, source_target_pairs={{0,1},{1,0},{2,3},{3,2},{4,5},{5,4},{6,7},{7,6},{8,9},{9,8},{10,11... | collective-permute-start | bytes 147464 | tf_op jit(solution)/shard_map/ppermute | solution.py:167
  4.4 2.6 %collective-permute-start.1 = (bf16[16,1536]{1,0:T(8,128)(2,1)S(1)}, bf16[16,1536]{1,0:T(8,128)(2,1)S(1)}, u32[]{:S(2)}, u32[]{:S(2)}) collective-permute-start(bf16[16,1536]{1,0:T(8,128)(2,1)S(1)} %get-tuple-element.23.refs_0_), channel_id=1, source_target_pairs={{0,2},{1,3},{2,0},{3,1},{4,6},{5,7},{6,4},{7,5},{8,10},{9,11},{10,... | collective-permute-start | bytes 147464 | tf_op jit(solution)/shard_map/ppermute | solution.py:167
  7.0 0.0 collective-permute-start.2
  7.0 0.0 collective-permute-done.refs_1_
  7.0 3.3 %collective-permute-done.1.refs_2_ = bf16[16,1536]{1,0:T(8,128)(2,1)S(1)} collective-permute-done((bf16[16,1536]{1,0:T(8,128)(2,1)S(1)}, bf16[16,1536]{1,0:T(8,128)(2,1)S(1)}, u32[]{:S(2)}, u32[]{:S(2)}) %collective-permute-start.1) | collective-permute-done | bytes 49184 | tf_op jit(solution)/shard_map/ppermute | solution.py:167
  10.3 2.6 %collective-permute-done.2.refs_3_ = bf16[16,1536]{1,0:T(8,128)(2,1)S(1)} collective-permute-done((bf16[16,1536]{1,0:T(8,128)(2,1)S(1)}, bf16[16,1536]{1,0:T(8,128)(2,1)S(1)}, u32[]{:S(2)}, u32[]{:S(2)}) %collective-permute-start.2) | collective-permute-done | bytes 49184 | tf_op jit(solution)/shard_map/ppermute | solution.py:167
  12.9 1.2 %shard_map.65 = (bf16[2,32,1024]{2,1,0:T(8,128)(2,1)S(1)}, bf16[2,32,1024]{2,1,0:T(8,128)(2,1)S(1)}, bf16[64,1536]{1,0:T(8,128)(2,1)S(1)}) custom-call(bf16[16,1536]{1,0:T(8,128)(2,1)S(1)} %get-tuple-element.23.refs_0_, bf16[16,1536]{1,0:T(8,128)(2,1)S(1)} %collective-permute-done.refs_1_, bf16[16,1536]{1,0:T(8,128)(2,1)S(1)} %collective-permute-done.1.refs_2_, ...), custom_call_target="tpu_custom_call" | custom-call | flops 402653184 | bytes 6291456 | tf_op jit(solution)/shard_map/pallas_call | solution.py:23
  14.1 0.1 collective-permute-start.12
  14.1 1.2 %shard_map.72 = (bf16[2,32,1024]{2,1,0:T(8,128)(2,1)S(1)}, bf16[2,32,1024]{2,1,0:T(8,128)(2,1)S(1)}) custom-call(bf16[64,1536]{1,0:T(8,128)(2,1)S(1)} %get-tuple-element.24.rows_ref, bf16[1536,4096]{1,0:T(8,128)(2,1)S(1)} %copy-done, bf16[1536,4096]{1,0:T(8,128)(2,1)S(1)} %copy-done.1), custom_call_target="tpu_custom_call" | custom-call | flops 402653184 | bytes 6291456 | tf_op jit(solution)/shard_map/pallas_call | solution.py:23
  15.4 0.0 slice-start
  15.4 0.0 slice-start.1
  15.4 1.2 %shard_map.69 = (bf16[2,32,1024]{2,1,0:T(8,128)(2,1)S(1)}, bf16[2,32,1024]{2,1,0:T(8,128)(2,1)S(1)}) custom-call(bf16[64,1536]{1,0:T(8,128)(2,1)S(1)} %get-tuple-element.24.rows_ref, bf16[1536,4096]{1,0:T(8,128)(2,1)S(1)} %copy-done, bf16[1536,4096]{1,0:T(8,128)(2,1)S(1)} %copy-done.1), custom_call_target="tpu_custom_call" | custom-call | flops 402653184 | bytes 6291456 | tf_op jit(solution)/shard_map/pallas_call | solution.py:23
  16.6 0.0 slice-start.2
  16.6 0.6 %collective-permute-start.9 = (bf16[2,32,1024]{2,1,0:T(8,128)(2,1)S(1)}, bf16[2,32,1024]{2,1,0:T(8,128)(2,1)S(1)}, u32[]{:S(2)}, u32[]{:S(2)}) collective-permute-start(bf16[2,32,1024]{2,1,0:T(8,128)(2,1)S(1)} %get-tuple-element.30), channel_id=1, source_target_pairs={{0,4},{4,0},{8,12},{12,8},{1,5},{5,1},{9,13},{13,9},{2,6},{6,2},{1... | collective-permute-start | bytes 393224 | tf_op jit(solution)/shard_map/ppermute | solution.py:167
  17.2 0.1 collective-permute-start.6
  17.2 1.2 %shard_map.66 = (bf16[2,32,1024]{2,1,0:T(8,128)(2,1)S(1)}, bf16[2,32,1024]{2,1,0:T(8,128)(2,1)S(1)}) custom-call(bf16[64,1536]{1,0:T(8,128)(2,1)S(1)} %get-tuple-element.24.rows_ref, bf16[1536,4096]{1,0:T(8,128)(2,1)S(1)} %copy-done, bf16[1536,4096]{1,0:T(8,128)(2,1)S(1)} %copy-done.1), custom_call_target="tpu_custom_call" | custom-call | flops 402653184 | bytes 6291456 | tf_op jit(solution)/shard_map/pallas_call | solution.py:23
  18.4 0.5 %collective-permute-start.3 = (bf16[2,32,1024]{2,1,0:T(8,128)(2,1)S(1)}, bf16[2,32,1024]{2,1,0:T(8,128)(2,1)S(1)}, u32[]{:S(2)}, u32[]{:S(2)}) collective-permute-start(bf16[2,32,1024]{2,1,0:T(8,128)(2,1)S(1)} %get-tuple-element.26), channel_id=1, source_target_pairs={{0,4},{4,0},{8,12},{12,8},{1,5},{5,1},{9,13},{13,9},{2,6},{6,2},{1... | collective-permute-start | bytes 393224 | tf_op jit(solution)/shard_map/ppermute | solution.py:167
  18.9 0.0 collective-permute-done.12.got_ref.pair_ref
  19.0 1.6 %collective-permute-start.13 = (bf16[2,32,1024]{2,1,0:T(8,128)(2,1)S(1)}, bf16[2,32,1024]{2,1,0:T(8,128)(2,1)S(1)}, u32[]{:S(2)}, u32[]{:S(2)}) collective-permute-start(bf16[2,32,1024]{2,1,0:T(8,128)(2,1)S(1)} %shard_map.75), channel_id=1, source_target_pairs={{0,8},{4,12},{8,0},{12,4},{1,9},{5,13},{9,1},{13,5},{2,10},{6,14},... | collective-permute-start | bytes 393224 | tf_op jit(solution)/shard_map/ppermute | solution.py:167
  20.5 0.0 collective-permute-done.9.got_ref.pair_ref
  20.6 0.6 %collective-permute-start.10 = (bf16[2,32,1024]{2,1,0:T(8,128)(2,1)S(1)}, bf16[2,32,1024]{2,1,0:T(8,128)(2,1)S(1)}, u32[]{:S(2)}, u32[]{:S(2)}) collective-permute-start(bf16[2,32,1024]{2,1,0:T(8,128)(2,1)S(1)} %shard_map.73), channel_id=1, source_target_pairs={{0,8},{4,12},{8,0},{12,4},{1,9},{5,13},{9,1},{13,5},{2,10},{6,14},... | collective-permute-start | bytes 393224 | tf_op jit(solution)/shard_map/ppermute | solution.py:167
  21.2 0.0 collective-permute-done.6.got_ref.pair_ref
  21.2 1.6 %collective-permute-start.7 = (bf16[2,32,1024]{2,1,0:T(8,128)(2,1)S(1)}, bf16[2,32,1024]{2,1,0:T(8,128)(2,1)S(1)}, u32[]{:S(2)}, u32[]{:S(2)}) collective-permute-start(bf16[2,32,1024]{2,1,0:T(8,128)(2,1)S(1)} %shard_map.70), channel_id=1, source_target_pairs={{0,8},{4,12},{8,0},{12,4},{1,9},{5,13},{9,1},{13,5},{2,10},{6,14},... | collective-permute-start | bytes 393224 | tf_op jit(solution)/shard_map/ppermute | solution.py:167
  22.8 0.0 collective-permute-done.3.got_ref.pair_ref
  22.8 0.6 %collective-permute-start.4 = (bf16[2,32,1024]{2,1,0:T(8,128)(2,1)S(1)}, bf16[2,32,1024]{2,1,0:T(8,128)(2,1)S(1)}, u32[]{:S(2)}, u32[]{:S(2)}) collective-permute-start(bf16[2,32,1024]{2,1,0:T(8,128)(2,1)S(1)} %shard_map.67), channel_id=1, source_target_pairs={{0,8},{4,12},{8,0},{12,4},{1,9},{5,13},{9,1},{13,5},{2,10},{6,14},... | collective-permute-start | bytes 393224 | tf_op jit(solution)/shard_map/ppermute | solution.py:167
  23.4 2.0 %collective-permute-done.13.cross_ref = bf16[2,32,1024]{2,1,0:T(8,128)(2,1)S(1)} collective-permute-done((bf16[2,32,1024]{2,1,0:T(8,128)(2,1)S(1)}, bf16[2,32,1024]{2,1,0:T(8,128)(2,1)S(1)}, u32[]{:S(2)}, u32[]{:S(2)}) %collective-permute-start.13) | collective-permute-done | bytes 131104 | tf_op jit(solution)/shard_map/ppermute | solution.py:167
  25.4 0.1 shard_map.76.mine_ref
  25.5 0.1 collective-permute-start.14
  25.6 2.6 %collective-permute-done.10.cross_ref = bf16[2,32,1024]{2,1,0:T(8,128)(2,1)S(1)} collective-permute-done((bf16[2,32,1024]{2,1,0:T(8,128)(2,1)S(1)}, bf16[2,32,1024]{2,1,0:T(8,128)(2,1)S(1)}, u32[]{:S(2)}, u32[]{:S(2)}) %collective-permute-start.10) | collective-permute-done | bytes 131104 | tf_op jit(solution)/shard_map/ppermute | solution.py:167
  28.2 0.1 shard_map.74.mine_ref
  28.3 0.1 collective-permute-start.11
  28.4 2.6 %collective-permute-done.7.cross_ref = bf16[2,32,1024]{2,1,0:T(8,128)(2,1)S(1)} collective-permute-done((bf16[2,32,1024]{2,1,0:T(8,128)(2,1)S(1)}, bf16[2,32,1024]{2,1,0:T(8,128)(2,1)S(1)}, u32[]{:S(2)}, u32[]{:S(2)}) %collective-permute-start.7) | collective-permute-done | bytes 131104 | tf_op jit(solution)/shard_map/ppermute | solution.py:167
  31.0 0.1 shard_map.71.mine_ref
  31.1 0.1 collective-permute-start.8
  31.2 1.8 %collective-permute-done.4.cross_ref = bf16[2,32,1024]{2,1,0:T(8,128)(2,1)S(1)} collective-permute-done((bf16[2,32,1024]{2,1,0:T(8,128)(2,1)S(1)}, bf16[2,32,1024]{2,1,0:T(8,128)(2,1)S(1)}, u32[]{:S(2)}, u32[]{:S(2)}) %collective-permute-start.4) | collective-permute-done | bytes 131104 | tf_op jit(solution)/shard_map/ppermute | solution.py:167
  32.9 0.1 shard_map.68.mine_ref
  33.0 0.1 collective-permute-start.5
  33.2 0.6 %shard_map.77.refs_0_ = f32[64,1536]{1,0:T(8,128)S(1)} custom-call(bf16[32,1024]{1,0:T(8,128)(2,1)S(1)} %shard_map.76.mine_ref, bf16[32,1024]{1,0:T(8,128)(2,1)S(1)} %collective-permute-done.14.beside_ref, bf16[4096,1536]{1,0:T(8,128)(2,1)S(1)} %bitcast.3), custom_call_target="tpu_custom_call" | custom-call | flops 201326592 | bytes 3145728 | tf_op jit(solution)/shard_map/pallas_call | solution.py:23
  33.8 0.0 collective-permute-done.11.beside_ref
  33.8 0.7 %shard_map.78.refs_0_ = f32[64,1536]{1,0:T(8,128)S(1)} custom-call(bf16[32,1024]{1,0:T(8,128)(2,1)S(1)} %shard_map.74.mine_ref, bf16[32,1024]{1,0:T(8,128)(2,1)S(1)} %collective-permute-done.11.beside_ref, bf16[4096,1536]{1,0:T(8,128)(2,1)S(1)} %bitcast.3, f32[64,1536]{1,0:T(8,128)S(1)} %shard_map.77.refs_0_), custom_call_target="tpu_custom_call" | custom-call | flops 201326592 | bytes 3145728 | tf_op jit(solution)/shard_map/pallas_call | solution.py:23
  34.5 0.7 %shard_map.79.total_ref = f32[64,1536]{1,0:T(8,128)S(1)} custom-call(bf16[32,1024]{1,0:T(8,128)(2,1)S(1)} %shard_map.71.mine_ref, bf16[32,1024]{1,0:T(8,128)(2,1)S(1)} %collective-permute-done.8.beside_ref, bf16[4096,1536]{1,0:T(8,128)(2,1)S(1)} %bitcast.3, f32[64,1536]{1,0:T(8,128)S(1)} %shard_map.78.refs_0_), custom_call_target="tpu_custom_call" | custom-call | flops 201326592 | bytes 3145728 | tf_op jit(solution)/shard_map/pallas_call | solution.py:23
  35.2 0.7 %shard_map.80 = (f32[16,1536]{1,0:T(8,128)S(1)}, bf16[16,1536]{1,0:T(8,128)(2,1)S(1)}, bf16[16,1536]{1,0:T(8,128)(2,1)S(1)}, bf16[16,1536]{1,0:T(8,128)(2,1)S(1)}) custom-call(bf16[32,1024]{1,0:T(8,128)(2,1)S(1)} %shard_map.68.mine_ref, bf16[32,1024]{1,0:T(8,128)(2,1)S(1)} %collective-permute-done.5.beside_ref, bf16[4096,1536]{1,0:T(8,128)(2,1)S(1)} %bitcast.3, ...), custom_call_target="tpu_custom_call" | custom-call | flops 201326592 | bytes 3145728 | tf_op jit(solution)/shard_map/pallas_call | solution.py:23
  35.9 0.1 collective-permute-start.15
  35.9 1.3 %collective-permute-start.16 = (bf16[16,1536]{1,0:T(8,128)(2,1)S(1)}, bf16[16,1536]{1,0:T(8,128)(2,1)S(1)}, u32[]{:S(2)}, u32[]{:S(2)}) collective-permute-start(bf16[16,1536]{1,0:T(8,128)(2,1)S(1)} %get-tuple-element.35), channel_id=1, source_target_pairs={{0,2},{1,3},{2,0},{3,1},{4,6},{5,7},{6,4},{7,5},{8,10},{9,11},{10,... | collective-permute-start | bytes 147464 | tf_op jit(solution)/shard_map/ppermute | solution.py:167
  37.2 3.1 %collective-permute-start.17 = (bf16[16,1536]{1,0:T(8,128)(2,1)S(1)}, bf16[16,1536]{1,0:T(8,128)(2,1)S(1)}, u32[]{:S(2)}, u32[]{:S(2)}) collective-permute-start(bf16[16,1536]{1,0:T(8,128)(2,1)S(1)} %get-tuple-element.36), channel_id=1, source_target_pairs={{0,3},{1,2},{2,1},{3,0},{4,7},{5,6},{6,5},{7,4},{8,11},{9,10},{10,... | collective-permute-start | bytes 147464 | tf_op jit(solution)/shard_map/ppermute | solution.py:167
  40.3 3.3 %collective-permute-done.16.refs_1_ = bf16[16,1536]{1,0:T(8,128)(2,1)S(1)} collective-permute-done((bf16[16,1536]{1,0:T(8,128)(2,1)S(1)}, bf16[16,1536]{1,0:T(8,128)(2,1)S(1)}, u32[]{:S(2)}, u32[]{:S(2)}) %collective-permute-start.16) | collective-permute-done | bytes 49184 | tf_op jit(solution)/shard_map/ppermute | solution.py:167
  43.6 0.8 %shard_map.81 = bf16[32,1536]{1,0:T(8,128)(2,1)} custom-call(bf16[32,96]{1,0:T(8,128)(2,1)S(1)} %get-tuple-element.21.slots_ref, f32[32,1]{1,0:T(8,128)S(1)} %get-tuple-element.22.combine_ref, f32[16,1536]{1,0:T(8,128)S(1)} %get-tuple-element.33.own_ref, bf16[16,1536]{1,0:T(8,128)(2,1)S(1)} %collective-permute-done.15.refs_0_, ...), custom_call_target="tpu_custom_call" | custom-call | flops 98304 | bytes 196608 | tf_op jit(solution)/shard_map/pallas_call | solution.py:23
  (17 shorter events, 0.2 us)
Async XLA Ops:
  0.0 12.9 %copy-start = (bf16[1536,4096]{1,0:T(8,128)(2,1)S(1)}, bf16[1536,4096]{1,0:T(8,128)(2,1)}, u32[]{:S(2)}) copy-start(bf16[1536,4096]{1,0:T(8,128)(2,1)} %gate_ref.5) | copy-start | bytes 37748740
  0.0 12.9 %copy-start.1 = (bf16[1536,4096]{1,0:T(8,128)(2,1)S(1)}, bf16[1536,4096]{1,0:T(8,128)(2,1)}, u32[]{:S(2)}) copy-start(bf16[1536,4096]{1,0:T(8,128)(2,1)} %up_ref.5) | copy-start | bytes 37748740
  1.3 5.7 %collective-permute-start = (bf16[16,1536]{1,0:T(8,128)(2,1)S(1)}, bf16[16,1536]{1,0:T(8,128)(2,1)S(1)}, u32[]{:S(2)}, u32[]{:S(2)}) collective-permute-start(bf16[16,1536]{1,0:T(8,128)(2,1)S(1)} %get-tuple-element.23.refs_0_), channel_id=1, source_target_pairs={{0,1},{1,0},{2,3},{3,2},{4,5},{5,4},{6,7},{7,6},{8,9},{9,8},{10,11... | collective-permute-start | bytes 147464 | tf_op jit(solution)/shard_map/ppermute | solution.py:167
  4.4 5.9 %collective-permute-start.1 = (bf16[16,1536]{1,0:T(8,128)(2,1)S(1)}, bf16[16,1536]{1,0:T(8,128)(2,1)S(1)}, u32[]{:S(2)}, u32[]{:S(2)}) collective-permute-start(bf16[16,1536]{1,0:T(8,128)(2,1)S(1)} %get-tuple-element.23.refs_0_), channel_id=1, source_target_pairs={{0,2},{1,3},{2,0},{3,1},{4,6},{5,7},{6,4},{7,5},{8,10},{9,11},{10,... | collective-permute-start | bytes 147464 | tf_op jit(solution)/shard_map/ppermute | solution.py:167
  7.0 5.9 %collective-permute-start.2 = (bf16[16,1536]{1,0:T(8,128)(2,1)S(1)}, bf16[16,1536]{1,0:T(8,128)(2,1)S(1)}, u32[]{:S(2)}, u32[]{:S(2)}) collective-permute-start(bf16[16,1536]{1,0:T(8,128)(2,1)S(1)} %get-tuple-element.23.refs_0_), channel_id=1, source_target_pairs={{0,3},{1,2},{2,1},{3,0},{4,7},{5,6},{6,5},{7,4},{8,11},{9,10},{10,... | collective-permute-start | bytes 147464 | tf_op jit(solution)/shard_map/ppermute | solution.py:167
  14.1 4.9 %collective-permute-start.12 = (bf16[2,32,1024]{2,1,0:T(8,128)(2,1)S(1)}, bf16[2,32,1024]{2,1,0:T(8,128)(2,1)S(1)}, u32[]{:S(2)}, u32[]{:S(2)}) collective-permute-start(bf16[2,32,1024]{2,1,0:T(8,128)(2,1)S(1)} %get-tuple-element.32), channel_id=1, source_target_pairs={{0,4},{4,0},{8,12},{12,8},{1,5},{5,1},{9,13},{13,9},{2,6},{6,2},{1... | collective-permute-start | bytes 393224 | tf_op jit(solution)/shard_map/ppermute | solution.py:167
  15.4 17.8 %slice-start = ((s8[12582912]{0:T(1024)(128)(4,1)}), s8[4194304]{0:T(1024)(128)(4,1)S(1)}, s32[]{:S(2)}) async-start(s8[12582912]{0:T(1024)(128)(4,1)} %bitcast.2), calls=%async_computation | async-start | bytes 8388608
  15.4 17.8 %slice-start.1 = ((s8[12582912]{0:T(1024)(128)(4,1)}), s8[4194304]{0:T(1024)(128)(4,1)S(1)}, s32[]{:S(2)}) async-start(s8[12582912]{0:T(1024)(128)(4,1)} %bitcast.2), calls=%async_computation.1 | async-start | bytes 8388608
  16.6 16.6 %slice-start.2 = ((s8[12582912]{0:T(1024)(128)(4,1)}), s8[4194304]{0:T(1024)(128)(4,1)S(1)}, s32[]{:S(2)}) async-start(s8[12582912]{0:T(1024)(128)(4,1)} %bitcast.2), calls=%async_computation.2 | async-start | bytes 8388608
  16.6 3.9 %collective-permute-start.9 = (bf16[2,32,1024]{2,1,0:T(8,128)(2,1)S(1)}, bf16[2,32,1024]{2,1,0:T(8,128)(2,1)S(1)}, u32[]{:S(2)}, u32[]{:S(2)}) collective-permute-start(bf16[2,32,1024]{2,1,0:T(8,128)(2,1)S(1)} %get-tuple-element.30), channel_id=1, source_target_pairs={{0,4},{4,0},{8,12},{12,8},{1,5},{5,1},{9,13},{13,9},{2,6},{6,2},{1... | collective-permute-start | bytes 393224 | tf_op jit(solution)/shard_map/ppermute | solution.py:167
  17.2 4.0 %collective-permute-start.6 = (bf16[2,32,1024]{2,1,0:T(8,128)(2,1)S(1)}, bf16[2,32,1024]{2,1,0:T(8,128)(2,1)S(1)}, u32[]{:S(2)}, u32[]{:S(2)}) collective-permute-start(bf16[2,32,1024]{2,1,0:T(8,128)(2,1)S(1)} %get-tuple-element.28), channel_id=1, source_target_pairs={{0,4},{4,0},{8,12},{12,8},{1,5},{5,1},{9,13},{13,9},{2,6},{6,2},{1... | collective-permute-start | bytes 393224 | tf_op jit(solution)/shard_map/ppermute | solution.py:167
  18.4 4.3 %collective-permute-start.3 = (bf16[2,32,1024]{2,1,0:T(8,128)(2,1)S(1)}, bf16[2,32,1024]{2,1,0:T(8,128)(2,1)S(1)}, u32[]{:S(2)}, u32[]{:S(2)}) collective-permute-start(bf16[2,32,1024]{2,1,0:T(8,128)(2,1)S(1)} %get-tuple-element.26), channel_id=1, source_target_pairs={{0,4},{4,0},{8,12},{12,8},{1,5},{5,1},{9,13},{13,9},{2,6},{6,2},{1... | collective-permute-start | bytes 393224 | tf_op jit(solution)/shard_map/ppermute | solution.py:167
  19.0 6.4 %collective-permute-start.13 = (bf16[2,32,1024]{2,1,0:T(8,128)(2,1)S(1)}, bf16[2,32,1024]{2,1,0:T(8,128)(2,1)S(1)}, u32[]{:S(2)}, u32[]{:S(2)}) collective-permute-start(bf16[2,32,1024]{2,1,0:T(8,128)(2,1)S(1)} %shard_map.75), channel_id=1, source_target_pairs={{0,8},{4,12},{8,0},{12,4},{1,9},{5,13},{9,1},{13,5},{2,10},{6,14},... | collective-permute-start | bytes 393224 | tf_op jit(solution)/shard_map/ppermute | solution.py:167
  20.6 7.6 %collective-permute-start.10 = (bf16[2,32,1024]{2,1,0:T(8,128)(2,1)S(1)}, bf16[2,32,1024]{2,1,0:T(8,128)(2,1)S(1)}, u32[]{:S(2)}, u32[]{:S(2)}) collective-permute-start(bf16[2,32,1024]{2,1,0:T(8,128)(2,1)S(1)} %shard_map.73), channel_id=1, source_target_pairs={{0,8},{4,12},{8,0},{12,4},{1,9},{5,13},{9,1},{13,5},{2,10},{6,14},... | collective-permute-start | bytes 393224 | tf_op jit(solution)/shard_map/ppermute | solution.py:167
  21.2 9.8 %collective-permute-start.7 = (bf16[2,32,1024]{2,1,0:T(8,128)(2,1)S(1)}, bf16[2,32,1024]{2,1,0:T(8,128)(2,1)S(1)}, u32[]{:S(2)}, u32[]{:S(2)}) collective-permute-start(bf16[2,32,1024]{2,1,0:T(8,128)(2,1)S(1)} %shard_map.70), channel_id=1, source_target_pairs={{0,8},{4,12},{8,0},{12,4},{1,9},{5,13},{9,1},{13,5},{2,10},{6,14},... | collective-permute-start | bytes 393224 | tf_op jit(solution)/shard_map/ppermute | solution.py:167
  22.8 10.1 %collective-permute-start.4 = (bf16[2,32,1024]{2,1,0:T(8,128)(2,1)S(1)}, bf16[2,32,1024]{2,1,0:T(8,128)(2,1)S(1)}, u32[]{:S(2)}, u32[]{:S(2)}) collective-permute-start(bf16[2,32,1024]{2,1,0:T(8,128)(2,1)S(1)} %shard_map.67), channel_id=1, source_target_pairs={{0,8},{4,12},{8,0},{12,4},{1,9},{5,13},{9,1},{13,5},{2,10},{6,14},... | collective-permute-start | bytes 393224 | tf_op jit(solution)/shard_map/ppermute | solution.py:167
  25.5 7.6 %collective-permute-start.14 = (bf16[32,1024]{1,0:T(8,128)(2,1)S(1)}, bf16[32,1024]{1,0:T(8,128)(2,1)S(1)}, u32[]{:S(2)}, u32[]{:S(2)}) collective-permute-start(bf16[32,1024]{1,0:T(8,128)(2,1)S(1)} %shard_map.76.mine_ref), channel_id=1, source_target_pairs={{0,4},{4,0},{8,12},{12,8},{1,5},{5,1},{9,13},{13,9},{2,6},{6,2},{1... | collective-permute-start | bytes 196616 | tf_op jit(solution)/shard_map/ppermute | solution.py:167
  28.3 5.5 %collective-permute-start.11 = (bf16[32,1024]{1,0:T(8,128)(2,1)S(1)}, bf16[32,1024]{1,0:T(8,128)(2,1)S(1)}, u32[]{:S(2)}, u32[]{:S(2)}) collective-permute-start(bf16[32,1024]{1,0:T(8,128)(2,1)S(1)} %shard_map.74.mine_ref), channel_id=1, source_target_pairs={{0,4},{4,0},{8,12},{12,8},{1,5},{5,1},{9,13},{13,9},{2,6},{6,2},{1... | collective-permute-start | bytes 196616 | tf_op jit(solution)/shard_map/ppermute | solution.py:167
  31.1 3.4 %collective-permute-start.8 = (bf16[32,1024]{1,0:T(8,128)(2,1)S(1)}, bf16[32,1024]{1,0:T(8,128)(2,1)S(1)}, u32[]{:S(2)}, u32[]{:S(2)}) collective-permute-start(bf16[32,1024]{1,0:T(8,128)(2,1)S(1)} %shard_map.71.mine_ref), channel_id=1, source_target_pairs={{0,4},{4,0},{8,12},{12,8},{1,5},{5,1},{9,13},{13,9},{2,6},{6,2},{1... | collective-permute-start | bytes 196616 | tf_op jit(solution)/shard_map/ppermute | solution.py:167
  33.0 2.1 %collective-permute-start.5 = (bf16[32,1024]{1,0:T(8,128)(2,1)S(1)}, bf16[32,1024]{1,0:T(8,128)(2,1)S(1)}, u32[]{:S(2)}, u32[]{:S(2)}) collective-permute-start(bf16[32,1024]{1,0:T(8,128)(2,1)S(1)} %shard_map.68.mine_ref), channel_id=1, source_target_pairs={{0,4},{4,0},{8,12},{12,8},{1,5},{5,1},{9,13},{13,9},{2,6},{6,2},{1... | collective-permute-start | bytes 196616 | tf_op jit(solution)/shard_map/ppermute | solution.py:167
  35.9 4.5 %collective-permute-start.15 = (bf16[16,1536]{1,0:T(8,128)(2,1)S(1)}, bf16[16,1536]{1,0:T(8,128)(2,1)S(1)}, u32[]{:S(2)}, u32[]{:S(2)}) collective-permute-start(bf16[16,1536]{1,0:T(8,128)(2,1)S(1)} %get-tuple-element.34), channel_id=1, source_target_pairs={{0,1},{1,0},{2,3},{3,2},{4,5},{5,4},{6,7},{7,6},{8,9},{9,8},{10,11... | collective-permute-start | bytes 147464 | tf_op jit(solution)/shard_map/ppermute | solution.py:167
  35.9 7.7 %collective-permute-start.16 = (bf16[16,1536]{1,0:T(8,128)(2,1)S(1)}, bf16[16,1536]{1,0:T(8,128)(2,1)S(1)}, u32[]{:S(2)}, u32[]{:S(2)}) collective-permute-start(bf16[16,1536]{1,0:T(8,128)(2,1)S(1)} %get-tuple-element.35), channel_id=1, source_target_pairs={{0,2},{1,3},{2,0},{3,1},{4,6},{5,7},{6,4},{7,5},{8,10},{9,11},{10,... | collective-permute-start | bytes 147464 | tf_op jit(solution)/shard_map/ppermute | solution.py:167
  37.2 6.4 %collective-permute-start.17 = (bf16[16,1536]{1,0:T(8,128)(2,1)S(1)}, bf16[16,1536]{1,0:T(8,128)(2,1)S(1)}, u32[]{:S(2)}, u32[]{:S(2)}) collective-permute-start(bf16[16,1536]{1,0:T(8,128)(2,1)S(1)} %get-tuple-element.36), channel_id=1, source_target_pairs={{0,3},{1,2},{2,1},{3,0},{4,7},{5,6},{6,5},{7,4},{8,11},{9,10},{10,... | collective-permute-start | bytes 147464 | tf_op jit(solution)/shard_map/ppermute | solution.py:167
